TPU v7x, 256 devices: a whole 4x4x8 slice. The times are simulated.
256 devices in a mesh: win: 4 (over z_hi), slab: 64 (over y, x, z_lo, core).
Axes of the slice: x: 4, y: 4, z: 8 (z_hi: 4, z_lo: 2; z = z_hi * 2 + z_lo), core: 2. Of those that a mesh axis runs over, the one named last changes fastest.
Arguments:
- lambdas: float32 [16], P('win'), parts along dimension 0, may hold values from 0 to 1
- charge_a: float32 [16, 32768], P('win', 'slab'), parts along dimension 0, may hold values from -3 to 3
- charge_b: float32 [16, 32768], P('win', 'slab'), parts along dimension 0, may hold values from -3 to 3
- perturbed: int32 [16, 32768], P('win', 'slab'), parts along dimension 0, may hold values 0 or 1
- grid_index: int32 [3, 16, 32768], P(None, 'win', 'slab'), parts along dimension 1, may hold values from 0 to 127, as said below
- spline_weights: float32 [3, 4, 16, 32768], P(None, None, 'win', 'slab'), parts along dimension 2, may hold values from 0 to 1, as said below
- spline_slopes: float32 [3, 4, 16, 32768], P(None, None, 'win', 'slab'), parts along dimension 2, may hold values from -1 to 1, as said below
Outputs:
- forces: float32 [3, 16, 32768], P(None, 'win', 'slab'), parts along dimension 1
- energy: float32 [16], P('win'), parts along dimension 0
- lambda_slope: float32 [16], P('win'), parts along dimension 0
There are 4 independent parts, one for each index of `win`. A program takes and returns all parts, laid end to end along the dimension named above; each array names one. Nothing has to cross between parts.
Inputs may be any that keep to these rules, and one draw needn't show every extreme that they name: `grid_index`: the z index of atom i lies in the planes of the slab index that holds it: from (i // 512) * 2 to that plus 2 - 1. `spline_weights`: along each dimension the four weights are the cubic B-spline values (1-u)^3/6, (3u^3-6u^2+4)/6, (-3u^3+3u^2+3u+1)/6, u^3/6 of the atom's fractional offset u in [0, 1). `spline_slopes`: the derivatives in u of spline_weights at the same offsets.
All inputs are finite; a program needn't handle non-finite values. No bound on the sum of `perturbed` on one device may be relied on, other than what follows from the above.
Results may differ from a plain program's by a relative error of at most 0.0003.
Values sent between devices are 32-bit elements; how exact they have to be, the bound alone decides.
No kernel may reach another device: no remote copies, remote signals or barrier semaphores. Data moves between devices by JAX's collectives and lax.ppermute only.
A program may use at most 64 MiB of HBM per device.

v0:
```python
import math

import jax
import jax.numpy as jnp
import numpy as np
from jax import lax
from jax.experimental import pallas as pl
from jax.experimental.pallas import tpu as pltpu
from jax.sharding import PartitionSpec as P

N = 128
WINDOWS = 4
HERE = 512
SLABS = 64
ATOMS = SLABS * HERE
high = lax.Precision.HIGH
gauss_width = 2.0


def blocks(real, imaginary):
    return np.block([[real, -imaginary], [imaginary, real]])


def tables():
    k = np.arange(N)
    angle = 2.0 * np.pi * ((k[:, None] * k[None, :]) % N) / N
    cosine, sine = np.cos(angle), np.sin(angle)
    forward = blocks(cosine, -sine)
    inverse = blocks(cosine, sine)
    order = np.arange(2 * N).reshape(2, N // 4, 4).transpose(1, 0, 2).ravel()
    return tuple(
        np.ascontiguousarray(m, dtype=np.float32)
        for m in (
            forward.T,
            forward[order],
            forward,
            inverse,
            inverse[:, order],
            inverse.T,
        )
    )


Y_FORWARD, X_FORWARD, Z_FORWARD, Z_INVERSE, X_INVERSE, Y_INVERSE = tables()


def dot(a, b):
    return jnp.dot(a, b, precision=high, preferred_element_type=jnp.float32)


def weights_of(u):
    v = 1.0 - u
    return (
        v * v * v * (1.0 / 6.0),
        (0.5 * u - 1.0) * u * u + (2.0 / 3.0),
        (0.5 * v - 1.0) * v * v + (2.0 / 3.0),
        u * u * u * (1.0 / 6.0),
    )


def slopes_of(u):
    v = 1.0 - u
    return (-0.5 * v * v, (1.5 * u - 2.0) * u, (2.0 - 1.5 * v) * v, 0.5 * u * u)


def pack_kernel(slab_ref, lambda_ref, a_ref, b_ref, flag_ref, index_ref, weight_ref, out_ref):
    flags = flag_ref[...].astype(jnp.float32)
    steps = flags * (b_ref[...] - a_ref[...])
    first = slab_ref[0] * 2
    out_ref[0] = index_ref[0].astype(jnp.float32)
    out_ref[1] = index_ref[1].astype(jnp.float32)
    out_ref[2] = (index_ref[2] - first).astype(jnp.float32)
    for axis in range(3):
        out_ref[3 + axis] = weight_ref[axis, 2] + 2.0 * weight_ref[axis, 3] - weight_ref[axis, 0]
    row = lax.broadcasted_iota(jnp.int32, (WINDOWS, HERE), 0)
    scale = jnp.zeros((WINDOWS, HERE), jnp.float32)
    for w in range(WINDOWS):
        scale = jnp.where(row == w, lambda_ref[w], scale)
    out_ref[6] = a_ref[...] + scale * steps
    out_ref[7] = steps


def cells(first):
    found = []
    for offset in range(4):
        cell = first + float(offset)
        found.append(jnp.where(cell >= float(N), cell - float(N), cell))
    return found


def spread_table(grid, targets, values):
    out = jnp.zeros(grid.shape, jnp.float32)
    for target, value in zip(targets, values):
        out = jnp.where(grid == target, value, out)
    return out


def plane_parts(source, plane, parts):
    low = plane < 0.5
    if source == 0:
        return jnp.where(low, parts[0], 0.0), jnp.where(low, parts[1], parts[0])
    if source == 1:
        return jnp.where(low, parts[2], parts[1]), jnp.where(low, parts[3], parts[2])
    return jnp.where(low, 0.0, parts[3]), None


def spread_kernel(own_ref, below_ref, far_ref, y_ref, x_ref, out_ref):
    grid = lax.broadcasted_iota(jnp.int32, (N, HERE), 0).astype(jnp.float32)
    planes = []
    for w in range(WINDOWS):
        total = [jnp.zeros((N, N), jnp.float32) for _ in range(2)]
        for source, ref in enumerate((own_ref, below_ref, far_ref)):
            row = lambda r: ref[r, w : w + 1, :]
            charge = row(6)
            depth = plane_parts(source, row(2), weights_of(row(5)))
            along_x = spread_table(grid, cells(row(0)), weights_of(row(3)))
            along_y = spread_table(grid, cells(row(1)), weights_of(row(4)))
            for p in range(2):
                if depth[p] is None:
                    continue
                total[p] = total[p] + lax.dot_general(
                    along_x,
                    along_y * (charge * depth[p]),
                    (((1,), (1,)), ((), ())),
                    precision=high,
                    preferred_element_type=jnp.float32,
                )
        planes.append(total)
    for c in range(2):
        for p in range(2):
            pair = jnp.concatenate([planes[2 * c][p], planes[2 * c + 1][p]], axis=1)
            rows = dot(pair, y_ref[...])
            column = dot(x_ref[...], jnp.concatenate([rows[:, :N], rows[:, N:]], axis=0))
            out_ref[c, :, p] = column.reshape(N // 4, 8, N)


def frequency(counter):
    return jnp.where(counter >= N // 2, counter - N, counter).astype(jnp.float32) / N


def column_kernel(slab_ref, in_ref, forward_ref, inverse_ref, out_ref):
    first = lax.rem(slab_ref[0], 32) * 4
    shape = (N, N)
    freq_z = frequency(lax.broadcasted_iota(jnp.int32, shape, 0))
    freq_y = frequency(lax.broadcasted_iota(jnp.int32, shape, 1))
    flat = freq_z * freq_z + freq_y * freq_y
    for j in range(4):
        freq_x = frequency(jnp.full(shape, first + j, jnp.int32))
        squared = flat + freq_x * freq_x
        positive = squared > 0
        safe = jnp.where(positive, squared, 1.0)
        influence = jnp.where(
            positive, jnp.exp(-gauss_width * squared) / (math.pi * N * N * N * safe), 0.0
        )
        both = jnp.concatenate(
            [in_ref[pl.ds(j, N, stride=8), :], in_ref[pl.ds(4 + j, N, stride=8), :]], axis=0
        )
        depth = dot(forward_ref[...], both)
        depth = depth * jnp.concatenate([influence, influence], axis=0)
        back = dot(inverse_ref[...], depth)
        out_ref[pl.ds(j, N, stride=8), :] = back[:N]
        out_ref[pl.ds(4 + j, N, stride=8), :] = back[N:]


def sample_kernel(
    in_ref, own_ref, below_ref, far_ref, x_ref, y_ref, own_out, below_out, far_out, sum_out
):
    grid = lax.broadcasted_iota(jnp.int32, (N, HERE), 0).astype(jnp.float32)
    planes = [[None, None] for _ in range(WINDOWS)]
    for c in range(2):
        for p in range(2):
            column = dot(x_ref[...], in_ref[c, :, p].reshape(2 * N, N))
            pair = dot(jnp.concatenate([column[:N], column[N:]], axis=1), y_ref[...])
            planes[2 * c][p] = pair[:, :N]
            planes[2 * c + 1][p] = pair[:, N:]
    lane = lax.broadcasted_iota(jnp.int32, (SLABS, N), 1)
    sums = jnp.zeros((SLABS, N), jnp.float32)
    for w in range(WINDOWS):
        energy = jnp.zeros((1, HERE), jnp.float32)
        slope = jnp.zeros((1, HERE), jnp.float32)
        for source, (ref, out_ref) in enumerate(
            ((own_ref, own_out), (below_ref, below_out), (far_ref, far_out))
        ):
            row = lambda r: ref[r, w : w + 1, :]
            charge = row(6)
            depth = plane_parts(source, row(2), weights_of(row(5)))
            steep = plane_parts(source, row(2), slopes_of(row(5)))
            at_x, at_y = cells(row(0)), cells(row(1))
            along_x = spread_table(grid, at_x, weights_of(row(3)))
            steep_x = spread_table(grid, at_x, slopes_of(row(3)))
            along_y = spread_table(grid, at_y, weights_of(row(4)))
            steep_y = spread_table(grid, at_y, slopes_of(row(4)))
            plain = over_z = over_y = None
            for p in range(2):
                if depth[p] is None:
                    continue
                level = dot(planes[w][p], along_y)
                level_y = dot(planes[w][p], steep_y)
                parts = (level * depth[p], level * steep[p], level_y * depth[p])
                if plain is None:
                    plain, over_z, over_y = parts
                else:
                    plain, over_z, over_y = plain + parts[0], over_z + parts[1], over_y + parts[2]
            potential = jnp.sum(along_x * plain, axis=0, keepdims=True)
            out_ref[0, w : w + 1, :] = -charge * jnp.sum(steep_x * plain, axis=0, keepdims=True)
            out_ref[1, w : w + 1, :] = -charge * jnp.sum(along_x * over_y, axis=0, keepdims=True)
            out_ref[2, w : w + 1, :] = -charge * jnp.sum(along_x * over_z, axis=0, keepdims=True)
            energy = energy + charge * potential
            slope = slope + row(7) * potential
        sums = jnp.where(lane == w, jnp.sum(energy, axis=1, keepdims=True), sums)
        sums = jnp.where(lane == WINDOWS + w, jnp.sum(slope, axis=1, keepdims=True), sums)
    sum_out[...] = sums


in_vmem = pl.BlockSpec(memory_space=pltpu.VMEM)
in_smem = pl.BlockSpec(memory_space=pltpu.SMEM)


def f32(*shape):
    return jax.ShapeDtypeStruct(shape, jnp.float32)


def passed_along(value, steps):
    pairs = [(source, (source + steps) % SLABS) for source in range(SLABS)]
    return lax.ppermute(value, "slab", pairs)


def body(lambdas, charge_a, charge_b, perturbed, grid_index, spline_weights, spline_slopes):
    slab = lax.axis_index("slab").reshape(1)
    own = pl.pallas_call(
        pack_kernel,
        out_shape=f32(8, WINDOWS, HERE),
        in_specs=[in_smem, in_smem] + [in_vmem] * 5,
        out_specs=in_vmem,
        name="pack",
    )(slab, lambdas, charge_a, charge_b, perturbed, grid_index, spline_weights)
    below = passed_along(own, 1)
    far = passed_along(own, 2)
    spectrum = pl.pallas_call(
        spread_kernel,
        out_shape=f32(2, N // 4, 2, 8, N),
        in_specs=[in_vmem] * 5,
        out_specs=in_vmem,
        name="spread",
    )(own, below, far, Y_FORWARD, X_FORWARD)
    columns = lax.all_to_all(spectrum.reshape(SLABS, 16, N), "slab", 0, 0, tiled=True)
    columns = pl.pallas_call(
        column_kernel,
        out_shape=f32(8 * N, N),
        in_specs=[in_smem] + [in_vmem] * 3,
        out_specs=in_vmem,
        name="columns",
    )(slab, columns.reshape(8 * N, N), Z_FORWARD, Z_INVERSE)
    levels = lax.all_to_all(columns.reshape(SLABS, 16, N), "slab", 0, 0, tiled=True)
    part = f32(3, WINDOWS, HERE)
    mine, for_below, for_far, sums = pl.pallas_call(
        sample_kernel,
        out_shape=(part, part, part, f32(SLABS, N)),
        in_specs=[in_vmem] * 6,
        out_specs=(in_vmem,) * 4,
        name="sample",
    )(levels.reshape(2, N // 4, 2, 8, N), own, below, far, X_INVERSE, Y_INVERSE)
    from_above = passed_along(for_below, -1)
    from_far = passed_along(for_far, -2)
    sums = lax.all_to_all(sums.reshape(SLABS, 1, N), "slab", 0, 0, tiled=True)
    sums = jnp.sum(sums, axis=(0, 1))
    return (
        mine + from_above + from_far,
        sums[:WINDOWS] * (0.5 / ATOMS),
        sums[WINDOWS : 2 * WINDOWS] * (1.0 / ATOMS),
    )


def solution(mesh):
    return jax.shard_map(
        body,
        mesh=mesh,
        in_specs=(
            P("win"),
            P("win", "slab"),
            P("win", "slab"),
            P("win", "slab"),
            P(None, "win", "slab"),
            P(None, None, "win", "slab"),
            P(None, None, "win", "slab"),
        ),
        out_specs=(P(None, "win", "slab"), P("win"), P("win")),
        check_vma=False,
    )
```

profile of v0, /device:TPU:1, one launch (start us, length us, event | category | flops | bytes accessed | tf_op | source)
XLA Modules:
  0.0 86.3 jit_solution(14067027420508324567)
XLA Ops:
  0.6 1.6 %pack.1.own_ref = f32[8,4,512]{2,1,0:T(4,128)} custom-call(s32[1]{0:T(128)} %bitcast.slab_ref, f32[4]{0:T(128)} %lambda_ref.1, f32[4,512]{1,0:T(4,128)} %a_ref.1, f32[4,512]{1,0:T(4,128)} %b_ref.1, s32[4,512]{1,0:T(4,128)} %flag_ref.1, s32[3,4,512]{2,1,0:T(4,128)} %index_ref.1, f32[3,4,4,512]{3,2,1,0:T(4,128)} %weight_ref.1), custom_call_target="tpu_custom_call" | custom-call | tf_op jit(solution)/shard_map/pack/pallas_call | solution.py:230
  2.2 2.5 %collective-permute-start.1 = (f32[8,4,512]{2,1,0:T(4,128)}, f32[8,4,512]{2,1,0:T(4,128)S(1)}, u32[]{:S(2)}, u32[]{:S(2)}) collective-permute-start(f32[8,4,512]{2,1,0:T(4,128)} %pack.1.own_ref), channel_id=1, source_target_pairs={{0,2},{1,3},{2,4},{3,5},{4,6},{5,7},{6,8},{7,9},{8,10},{9,11},{10,... | collective-permute-start | bytes 196616 | tf_op jit(solution)/shard_map/ppermute | solution.py:225
  4.7 1.6 %collective-permute-start = (f32[8,4,512]{2,1,0:T(4,128)}, f32[8,4,512]{2,1,0:T(4,128)S(1)}, u32[]{:S(2)}, u32[]{:S(2)}) collective-permute-start(f32[8,4,512]{2,1,0:T(4,128)} %pack.1.own_ref), channel_id=1, source_target_pairs={{0,1},{1,2},{2,3},{3,4},{4,5},{5,6},{6,7},{7,8},{8,9},{9,10},{10,1... | collective-permute-start | bytes 196616 | tf_op jit(solution)/shard_map/ppermute | solution.py:225
  6.3 4.9 %collective-permute-done.1.far_ref = f32[8,4,512]{2,1,0:T(4,128)S(1)} collective-permute-done((f32[8,4,512]{2,1,0:T(4,128)}, f32[8,4,512]{2,1,0:T(4,128)S(1)}, u32[]{:S(2)}, u32[]{:S(2)}) %collective-permute-start.1) | collective-permute-done | bytes 65568 | tf_op jit(solution)/shard_map/ppermute | solution.py:225
  11.2 0.0 copy-start
  11.2 0.0 collective-permute-done.below_ref
  11.2 0.6 copy-done
  11.8 0.0 copy-start.1
  11.8 0.6 copy-done.1
  12.5 6.2 %spread.1 = f32[2,32,2,8,128]{4,3,2,1,0:T(8,128)} custom-call(f32[8,4,512]{2,1,0:T(4,128)} %pack.1.own_ref, f32[8,4,512]{2,1,0:T(4,128)} %copy-done.1, f32[8,4,512]{2,1,0:T(4,128)} %copy-done, f32[256,256]{1,0:T(8,128)} %constant.18.clone.y_ref.inverse_ref, f32[256,256]{1,0:T(8,128)} %constant.19.clone.x_ref), custom_call_target="tpu_custom_call" | custom-call | tf_op jit(solution)/shard_map/spread/pallas_call | solution.py:239
  18.7 21.0 %all_to_all.15 = f32[64,16,128]{2,1,0:T(8,128)} all-to-all(f32[64,16,128]{2,1,0:T(8,128)} %bitcast.11), channel_id=1, replica_groups=mesh['win'=4,'slab'=64] {'slab'}, dimensions={0} | all-to-all | bytes 1048576 | tf_op jit(solution)/shard_map/all_to_all | solution.py:246
  39.6 3.3 %columns.1 = f32[1024,128]{1,0:T(8,128)} custom-call(s32[1]{0:T(128)} %bitcast.slab_ref, f32[1024,128]{1,0:T(8,128)} %bitcast.9, f32[256,256]{1,0:T(8,128)} %constant.20.clone.forward_ref.y_ref, f32[256,256]{1,0:T(8,128)} %constant.18.clone.y_ref.inverse_ref), custom_call_target="tpu_custom_call" | custom-call | tf_op jit(solution)/shard_map/columns/pallas_call | solution.py:247
  42.9 18.2 %all_to_all.16 = f32[64,16,128]{2,1,0:T(8,128)} all-to-all(f32[64,16,128]{2,1,0:T(8,128)} %bitcast.10), channel_id=1, replica_groups=mesh['win'=4,'slab'=64] {'slab'}, dimensions={0} | all-to-all | bytes 1048576 | tf_op jit(solution)/shard_map/all_to_all | solution.py:254
  61.1 10.1 %sample.1 = (f32[3,4,512]{2,1,0:T(4,128)}, f32[3,4,512]{2,1,0:T(4,128)}, f32[3,4,512]{2,1,0:T(4,128)}, f32[64,128]{1,0:T(8,128)}) custom-call(f32[2,32,2,8,128]{4,3,2,1,0:T(8,128)} %bitcast.8, f32[8,4,512]{2,1,0:T(4,128)} %pack.1.own_ref, f32[8,4,512]{2,1,0:T(4,128)} %copy-done.1, f32[8,4,512]{2,1,0:T(4,128)} %copy-done, f32[256,256]{1,0:T(8,128)} %constant.21.clone.x_ref, ...), custom_call_target="tpu_custom_call" | custom-call | tf_op jit(solution)/shard_map/sample/pallas_call | solution.py:256
  71.1 0.5 collective-permute-start.2
  71.6 0.9 %collective-permute-start.3 = (f32[3,4,512]{2,1,0:T(4,128)}, f32[3,4,512]{2,1,0:T(4,128)S(1)}, u32[]{:S(2)}, u32[]{:S(2)}) collective-permute-start(f32[3,4,512]{2,1,0:T(4,128)} %get-tuple-element.9), channel_id=1, source_target_pairs={{0,62},{1,63},{2,0},{3,1},{4,2},{5,3},{6,4},{7,5},{8,6},{9,7},{10,... | collective-permute-start | bytes 73736 | tf_op jit(solution)/shard_map/ppermute | solution.py:225
  72.5 0.0 copy-start.2
  72.5 5.2 %all-to-all-start.2 = ((f32[64,1,128]{2,1,0:T(1,128)}), f32[64,1,128]{2,1,0:T(1,128)S(1)}, u32[]{:S(2)}, u32[]{:S(2)}) async-start(f32[64,1,128]{2,1,0:T(1,128)} %bitcast.12), calls=%async_computation.2 | async-start | bytes 65536 | tf_op jit(solution)/shard_map/all_to_all | solution.py:265
  77.7 0.0 collective-permute-done.2
  77.7 0.0 collective-permute-done.3
  77.7 0.0 copy-done.2
  77.8 0.6 add_add_fusion
  78.4 7.2 %all-to-all-done.2 = f32[64,1,128]{2,1,0:T(1,128)S(1)} async-done(((f32[64,1,128]{2,1,0:T(1,128)}), f32[64,1,128]{2,1,0:T(1,128)S(1)}, u32[]{:S(2)}, u32[]{:S(2)}) %all-to-all-start.2) | async-done | bytes 32800 | tf_op jit(solution)/shard_map/all_to_all | solution.py:265
  85.6 0.1 reduce_sum.9
  85.7 0.6 slice_multiply_fusion
Async XLA Ops:
  2.2 9.0 %collective-permute-start.1 = (f32[8,4,512]{2,1,0:T(4,128)}, f32[8,4,512]{2,1,0:T(4,128)S(1)}, u32[]{:S(2)}, u32[]{:S(2)}) collective-permute-start(f32[8,4,512]{2,1,0:T(4,128)} %pack.1.own_ref), channel_id=1, source_target_pairs={{0,2},{1,3},{2,4},{3,5},{4,6},{5,7},{6,8},{7,9},{8,10},{9,11},{10,... | collective-permute-start | bytes 196616 | tf_op jit(solution)/shard_map/ppermute | solution.py:225
  4.7 6.5 %collective-permute-start = (f32[8,4,512]{2,1,0:T(4,128)}, f32[8,4,512]{2,1,0:T(4,128)S(1)}, u32[]{:S(2)}, u32[]{:S(2)}) collective-permute-start(f32[8,4,512]{2,1,0:T(4,128)} %pack.1.own_ref), channel_id=1, source_target_pairs={{0,1},{1,2},{2,3},{3,4},{4,5},{5,6},{6,7},{7,8},{8,9},{9,10},{10,1... | collective-permute-start | bytes 196616 | tf_op jit(solution)/shard_map/ppermute | solution.py:225
  11.2 0.6 copy-start
  11.8 0.6 copy-start.1
  71.1 6.6 %collective-permute-start.2 = (f32[3,4,512]{2,1,0:T(4,128)}, f32[3,4,512]{2,1,0:T(4,128)S(1)}, u32[]{:S(2)}, u32[]{:S(2)}) collective-permute-start(f32[3,4,512]{2,1,0:T(4,128)} %get-tuple-element.8), channel_id=1, source_target_pairs={{0,63},{1,0},{2,1},{3,2},{4,3},{5,4},{6,5},{7,6},{8,7},{9,8},{10,9... | collective-permute-start | bytes 73736 | tf_op jit(solution)/shard_map/ppermute | solution.py:225
  71.6 6.1 %collective-permute-start.3 = (f32[3,4,512]{2,1,0:T(4,128)}, f32[3,4,512]{2,1,0:T(4,128)S(1)}, u32[]{:S(2)}, u32[]{:S(2)}) collective-permute-start(f32[3,4,512]{2,1,0:T(4,128)} %get-tuple-element.9), channel_id=1, source_target_pairs={{0,62},{1,63},{2,0},{3,1},{4,2},{5,3},{6,4},{7,5},{8,6},{9,7},{10,... | collective-permute-start | bytes 73736 | tf_op jit(solution)/shard_map/ppermute | solution.py:225
  72.5 5.3 %copy-start.2 = (f32[3,4,512]{2,1,0:T(4,128)S(1)}, f32[3,4,512]{2,1,0:T(4,128)}, u32[]{:S(2)}) copy-start(f32[3,4,512]{2,1,0:T(4,128)} %get-tuple-element.7) | copy-start | bytes 73732
  72.5 13.1 %all-to-all-start.2 = ((f32[64,1,128]{2,1,0:T(1,128)}), f32[64,1,128]{2,1,0:T(1,128)S(1)}, u32[]{:S(2)}, u32[]{:S(2)}) async-start(f32[64,1,128]{2,1,0:T(1,128)} %bitcast.12), calls=%async_computation.2 | async-start | bytes 65536 | tf_op jit(solution)/shard_map/all_to_all | solution.py:265
where the time goes:
time: 86.7 us; the launch traced here: 86.3 us
  blocking collectives  39.1 us (45%)
  Pallas kernels  21.2 us (24%)
  waiting for transfers between devices  12.2 us (14%)
  starting transfers between devices  10.6 us (12%)
  other arithmetic  1.29 us (1%)
  local copies, waits for them, and re-layouts  1.25 us (1%)
    all_to_all x1, blocking collectives, body(): lax.all_to_all(spectrum.reshape(SLABS, 16, N), 'slab', 0, 0, tiled=True)  21 us
    all_to_all x1, blocking collectives, body(): lax.all_to_all(columns.reshape(SLABS, 16, N), 'slab', 0, 0, tiled=True)  18.2 us
    pallas_call x1, Pallas kernels, body(): pl.pallas_call(sample_kernel, out_shape=(part, part, part, f32(SLABS, N))...  10.1 us
    all_to_all x1, waiting for transfers between devices, body(): sums = lax.all_to_all(sums.reshape(SLABS, 1, N), 'slab', 0, 0, tiled=True)  7.24 us
    pallas_call x1, Pallas kernels, body(): pl.pallas_call(spread_kernel, out_shape=f32(2, N // 4, 2, 8, N), in_specs...  6.21 us
    ppermute x4, starting transfers between devices, passed_along(): return lax.ppermute(value, 'slab', pairs)  5.4 us
    all_to_all x1, starting transfers between devices, body(): sums = lax.all_to_all(sums.reshape(SLABS, 1, N), 'slab', 0, 0, tiled=True)  5.22 us
    ppermute x4, waiting for transfers between devices, passed_along(): return lax.ppermute(value, 'slab', pairs)  4.92 us
  transfers between devices with their start and end apart: 5, of which 2 were waited for; matrix products, arithmetic and copies ran while one was open for 1% of the time, Pallas kernels for 0%

commit v1 on v0

v1 whole, which is shorter than its diff:
```python
import math

import jax
import jax.numpy as jnp
import numpy as np
from jax import lax
from jax.experimental import pallas as pl
from jax.experimental.pallas import tpu as pltpu
from jax.sharding import PartitionSpec as P

N = 128
LANES = 128
WINDOWS = 4
HERE = 512
SLABS = 64
ATOMS = SLABS * HERE
gauss_width = 2.0


def blocks(real, imaginary):
    return np.block([[real, -imaginary], [imaginary, real]])


def tables():
    k = np.arange(N)
    angle = 2.0 * np.pi * ((k[:, None] * k[None, :]) % N) / N
    cosine, sine = np.cos(angle), np.sin(angle)
    forward = blocks(cosine, -sine)
    inverse = blocks(cosine, sine)
    order = np.arange(2 * N).reshape(2, N // 4, 4).transpose(1, 0, 2).ravel()
    return tuple(
        np.ascontiguousarray(m, dtype=np.float32)
        for m in (
            forward.T,
            forward[order],
            forward,
            inverse,
            inverse[:, order],
            inverse.T,
        )
    )


def halves(x):
    top = x.astype(jnp.bfloat16)
    return top, (x - top.astype(jnp.float32)).astype(jnp.bfloat16)


def table_halves(table):
    top = table.astype(jnp.bfloat16)
    return np.stack([top, (table - top.astype(np.float32)).astype(jnp.bfloat16)])


Y_FORWARD, X_FORWARD, Z_FORWARD, Z_INVERSE, X_INVERSE, Y_INVERSE = map(table_halves, tables())


def dot(a, b, contract=(1, 0)):
    dims = (((contract[0],), (contract[1],)), ((), ()))
    return lax.dot_general(a, b, dims, preferred_element_type=jnp.float32)


def table_times(table_ref, x):
    top, rest = halves(x)
    return dot(table_ref[0], top) + dot(table_ref[1], top) + dot(table_ref[0], rest)


def times_table(x, table_ref):
    top, rest = halves(x)
    return dot(top, table_ref[0]) + dot(rest, table_ref[0]) + dot(top, table_ref[1])


def weights_of(u):
    v = 1.0 - u
    return (
        v * v * v * (1.0 / 6.0),
        (0.5 * u - 1.0) * u * u + (2.0 / 3.0),
        (0.5 * v - 1.0) * v * v + (2.0 / 3.0),
        u * u * u * (1.0 / 6.0),
    )


def slopes_of(u):
    v = 1.0 - u
    return (-0.5 * v * v, (1.5 * u - 2.0) * u, (2.0 - 1.5 * v) * v, 0.5 * u * u)


def pack_kernel(slab_ref, *refs):
    sources, out_ref, landed, sem = refs[:6], refs[6], refs[7:13], refs[13]
    copies = [
        pltpu.make_async_copy(source, target, sem.at[i])
        for i, (source, target) in enumerate(zip(sources, landed))
    ]
    for copy in copies:
        copy.start()
    for copy in copies:
        copy.wait()
    lambda_ref, a_ref, b_ref, flag_ref, index_ref, weight_ref = landed
    flags = flag_ref[...].astype(jnp.float32)
    steps = flags * (b_ref[...] - a_ref[...])
    first = slab_ref[0] * 2
    out_ref[0] = index_ref[0].astype(jnp.float32)
    out_ref[1] = index_ref[1].astype(jnp.float32)
    out_ref[2] = (index_ref[2] - first).astype(jnp.float32)
    for axis in range(3):
        out_ref[3 + axis] = weight_ref[axis, 2] + 2.0 * weight_ref[axis, 3] - weight_ref[axis, 0]
    row = lax.broadcasted_iota(jnp.int32, (WINDOWS, HERE), 0)
    scale = jnp.zeros((WINDOWS, HERE), jnp.float32)
    for w in range(WINDOWS):
        scale = jnp.where(row == w, lambda_ref[w], scale)
    out_ref[6] = a_ref[...] + scale * steps
    out_ref[7] = steps


def places(first, height):
    block = jnp.floor(first * (1.0 / height))
    after = jnp.where(block == float(N // height - 1), 0.0, block + 1.0)
    return block, after, first - height * block


def row_halves(value):
    top = value.astype(jnp.bfloat16).astype(jnp.float32)
    return top, value - top


def wide(row):
    return jnp.broadcast_to(row, (16, LANES)).astype(jnp.bfloat16)


def tall(row):
    return jnp.broadcast_to(row, (8, LANES))


def rows_of(height):
    return lax.broadcasted_iota(jnp.int32, (height, LANES), 0).astype(jnp.float32)


def stencil_tiles(rows, height, start, columns):
    zero = jnp.zeros_like(rows)
    here = [rows == start + jnp.asarray(k, rows.dtype) for k in range(4)]
    past = [rows + jnp.asarray(height, rows.dtype) == start + jnp.asarray(k, rows.dtype) for k in range(1, 4)]
    tiles = []
    for values in columns:
        first = second = zero
        for k in range(4):
            first = jnp.where(here[k], values[k], first)
        for k in range(1, 4):
            second = jnp.where(past[k - 1], values[k], second)
        tiles.append((first, second))
    return tiles


def table_columns(block, after, tiles):
    columns = [[] for _ in tiles]
    zero = jnp.zeros_like(tiles[0][0])
    for b in range(N // 16):
        at, next_at = block == jnp.asarray(b, block.dtype), after == jnp.asarray(b, block.dtype)
        for column, (first, second) in zip(columns, tiles):
            column.append(jnp.where(at, first, jnp.where(next_at, second, zero)))
    return [jnp.concatenate(column, axis=0) for column in columns]


def plane_parts(source, plane, parts):
    low = plane < 0.5
    if source == 0:
        return jnp.where(low, parts[0], 0.0), jnp.where(low, parts[1], parts[0])
    if source == 1:
        return jnp.where(low, parts[2], parts[1]), jnp.where(low, parts[3], parts[2])
    return jnp.where(low, 0.0, parts[3]), None


def spread_rows(source, ref, keep):
    block, after, row = places(ref[0], 16)
    keep[0], keep[1], keep[2] = block, after, row
    block, after, row = places(ref[1], 16)
    keep[3], keep[4], keep[5] = block, after, row
    for k, value in enumerate(weights_of(ref[3])):
        keep[6 + k], keep[10 + k] = row_halves(value)
    along_y = weights_of(ref[4])
    for p, depth in enumerate(plane_parts(source, ref[2], weights_of(ref[5]))):
        if depth is not None:
            for k in range(4):
                top, rest = row_halves(along_y[k] * (ref[6] * depth))
                keep[14 + 8 * p + k], keep[18 + 8 * p + k] = top, rest


def spread_planes(sources, keep):
    for slot, (source, ref) in enumerate(sources):
        spread_rows(source, ref, keep.at[slot])
    rows16 = rows_of(16).astype(jnp.bfloat16)
    blank = jnp.zeros((N, LANES), jnp.bfloat16)
    planes = []
    for w in range(WINDOWS):
        left, right_top, right_rest = [], [], []
        for slot, (source, ref) in enumerate(sources):
            for chunk in range(HERE // LANES):
                lanes = slice(chunk * LANES, (chunk + 1) * LANES)
                row = lambda r: wide(keep[slot, r, w : w + 1, lanes])
                four = lambda r: [row(r + k) for k in range(4)]
                tiles = stencil_tiles(rows16, 16, row(2), [four(6), four(10)])
                left.append(jnp.concatenate(table_columns(row(0), row(1), tiles), axis=0))
                count = 1 if source == 2 else 2
                tiles = stencil_tiles(
                    rows16, 16, row(5), [four(14 + 4 * i) for i in range(2 * count)]
                )
                found = table_columns(row(3), row(4), tiles)
                if count == 1:
                    found = found + [blank, blank]
                right_top.append(jnp.concatenate([found[0], found[2]], axis=0))
                right_rest.append(jnp.concatenate([found[1], found[3]], axis=0))
        left = jnp.concatenate(left, axis=1)
        both = dot(left, jnp.concatenate(right_top, axis=1), (1, 1))
        rest = dot(left[:N], jnp.concatenate(right_rest, axis=1), (1, 1))
        planes.append(both[:N] + both[N:] + rest)
    return planes


def own_spread_kernel(own_ref, out_ref, keep):
    for w, planes in enumerate(spread_planes(((0, own_ref),), keep)):
        out_ref[w] = planes


def spread_kernel(own_ref, below_ref, far_ref, y_hbm, x_hbm, out_ref, keep, y_ref, x_ref, sem):
    copies = [
        pltpu.make_async_copy(y_hbm, y_ref, sem.at[0]),
        pltpu.make_async_copy(x_hbm, x_ref, sem.at[1]),
    ]
    for copy in copies:
        copy.start()
    planes = spread_planes(((1, below_ref), (2, far_ref)), keep)
    planes = [own_ref[w] + planes[w] for w in range(WINDOWS)]
    for copy in copies:
        copy.wait()
    stacked = jnp.concatenate(
        [
            jnp.concatenate([planes[2 * c][:, cut], planes[2 * c + 1][:, cut]], axis=1)
            for c in range(2)
            for cut in (slice(0, N), slice(N, 2 * N))
        ],
        axis=0,
    )
    turned = times_table(stacked, y_ref)
    upright = jnp.concatenate(
        [
            jnp.concatenate([turned[b * N : b * N + N, :N], turned[b * N : b * N + N, N:]], axis=0)
            for b in range(4)
        ],
        axis=1,
    )
    columns = table_times(x_ref, upright)
    for b in range(4):
        out_ref[b // 2, :, b % 2] = columns[:, b * N : b * N + N].reshape(N // 4, 8, N)


def frequency(counter):
    return jnp.where(counter >= N // 2, counter - N, counter).astype(jnp.float32) / N


def influence_kernel(slab_ref, out_ref):
    first = lax.rem(slab_ref[0], SLABS // 2) * 4
    shape = (N, N)
    freq_z = frequency(lax.broadcasted_iota(jnp.int32, shape, 0))
    freq_y = frequency(lax.broadcasted_iota(jnp.int32, shape, 1))
    flat = freq_z * freq_z + freq_y * freq_y
    for j in range(4):
        freq_x = frequency(jnp.full(shape, first + j, jnp.int32))
        squared = flat + freq_x * freq_x
        positive = squared > 0
        safe = jnp.where(positive, squared, 1.0)
        out_ref[:, j * N : j * N + N] = jnp.where(
            positive, jnp.exp(-gauss_width * squared) / (math.pi * N * N * N * safe), 0.0
        )


def column_kernel(in_ref, influence_ref, forward_ref, inverse_ref, out_ref):
    part = lambda r: in_ref[pl.ds(r, N, stride=8), :]
    columns = jnp.concatenate(
        [jnp.concatenate([part(j), part(4 + j)], axis=0) for j in range(4)], axis=1
    )
    depth = table_times(forward_ref, columns)
    influence = influence_ref[...]
    depth = jnp.concatenate([depth[:N] * influence, depth[N:] * influence], axis=0)
    back = table_times(inverse_ref, depth)
    for j in range(4):
        out_ref[pl.ds(j, N, stride=8), :] = back[:N, j * N : j * N + N]
        out_ref[pl.ds(4 + j, N, stride=8), :] = back[N:, j * N : j * N + N]


def sample_rows(source, ref, keep):
    block, after, row = places(ref[1], 16)
    keep[0], keep[1], keep[2] = block, after, row
    for k, value in enumerate(weights_of(ref[4])):
        keep[3 + k], keep[7 + k] = row_halves(value)
    for k, value in enumerate(slopes_of(ref[4])):
        keep[11 + k], keep[15 + k] = row_halves(value)
    block, after, row = places(ref[0], 8)
    keep[19], keep[20], keep[21] = block, after, row
    for k, (value, slope) in enumerate(zip(weights_of(ref[3]), slopes_of(ref[3]))):
        keep[22 + k], keep[26 + k] = value, slope
    depth = plane_parts(source, ref[2], weights_of(ref[5]))
    steep = plane_parts(source, ref[2], slopes_of(ref[5]))
    for p in range(2):
        if depth[p] is not None:
            keep[30 + p], keep[32 + p] = depth[p], steep[p]


def sample_kernel(
    in_ref, own_ref, below_ref, far_ref, x_ref, y_ref, own_out, below_out, far_out, sum_out, keep, sums
):
    sources = ((0, own_ref, own_out), (1, below_ref, below_out), (2, far_ref, far_out))
    columns = jnp.concatenate(
        [in_ref[b // 2, :, b % 2].reshape(2 * N, N) for b in range(4)], axis=1
    )
    upright = table_times(x_ref, columns)
    flat = jnp.concatenate(
        [
            jnp.concatenate([upright[:N, b * N : b * N + N], upright[N:, b * N : b * N + N]], axis=1)
            for b in range(4)
        ],
        axis=0,
    )
    pairs = times_table(flat, y_ref)
    for source, ref, _ in sources:
        sample_rows(source, ref, keep.at[source])
    rows16 = rows_of(16).astype(jnp.bfloat16)
    rows8 = rows_of(8)
    for w in range(WINDOWS):
        side = slice((w % 2) * N, (w % 2) * N + N)
        start = (w // 2) * 2 * N
        planes = jnp.concatenate(halves(pairs[start : start + 2 * N, side]), axis=1)
        energy = jnp.zeros((1, LANES), jnp.float32)
        slope = jnp.zeros((1, LANES), jnp.float32)
        for source, ref, out_ref in sources:
            tops, rests = [], []
            for chunk in range(HERE // LANES):
                lanes = slice(chunk * LANES, (chunk + 1) * LANES)
                row = lambda r: wide(keep[source, r, w : w + 1, lanes])
                four = lambda r: [row(r + k) for k in range(4)]
                tiles = stencil_tiles(rows16, 16, row(2), [four(3 + 4 * i) for i in range(4)])
                found = table_columns(row(0), row(1), tiles)
                tops.append(jnp.concatenate([found[0], found[2]], axis=1))
                rests.append(jnp.concatenate([found[1], found[3]], axis=1))
            count = 1 if source == 2 else 2
            tops = jnp.concatenate(tops, axis=1)
            rests = jnp.concatenate(rests, axis=1)
            used = planes[: count * N]
            levels = dot(used, jnp.concatenate([tops, tops], axis=0)) + dot(used[:, :N], rests)
            for chunk in range(HERE // LANES):
                lanes = slice(chunk * LANES, (chunk + 1) * LANES)
                row = lambda r: tall(keep[source, r, w : w + 1, lanes])
                four = lambda r: [row(r + k) for k in range(4)]
                block, after = row(19), row(20)
                tiles = stencil_tiles(rows8, 8, row(21), [four(22), four(26)])
                near = [[None] * 2 for _ in range(2 * count)]
                for b in range(N // 8):
                    at, next_at = block == float(b), after == float(b)
                    for q in range(2 * count):
                        p, kind = q // 2, q % 2
                        level = levels[
                            p * N + b * 8 : p * N + b * 8 + 8,
                            (2 * chunk + kind) * LANES : (2 * chunk + kind + 1) * LANES,
                        ]
                        if b == 0:
                            near[q] = [level, level]
                        else:
                            near[q][0] = jnp.where(at, level, near[q][0])
                            near[q][1] = jnp.where(next_at, level, near[q][1])
                total = [jnp.zeros((8, LANES), jnp.float32) for _ in range(4)]
                for half in range(2):
                    along, along_dx = tiles[0][half], tiles[1][half]
                    plain = near[0][half] * row(30)
                    over_z = near[0][half] * row(32)
                    over_y = near[1][half] * row(30)
                    if count == 2:
                        plain = plain + near[2][half] * row(31)
                        over_z = over_z + near[2][half] * row(33)
                        over_y = over_y + near[3][half] * row(31)
                    total[0] = total[0] + along * plain
                    total[1] = total[1] + along_dx * plain
                    total[2] = total[2] + along * over_y
                    total[3] = total[3] + along * over_z
                total = [jnp.sum(t, axis=0, keepdims=True) for t in total]
                charge = ref[6, w : w + 1, lanes]
                for d in range(3):
                    out_ref[d, w : w + 1, lanes] = -charge * total[1 + d]
                energy = energy + charge * total[0]
                slope = slope + ref[7, w : w + 1, lanes] * total[0]
        sums[w : w + 1, :] = energy
        sums[WINDOWS + w : WINDOWS + w + 1, :] = slope
    added = jnp.sum(sums[...], axis=1, keepdims=True)
    shape = (8, LANES)
    here = lax.broadcasted_iota(jnp.int32, shape, 0) == lax.broadcasted_iota(jnp.int32, shape, 1)
    line = jnp.sum(jnp.where(here, added, 0.0), axis=0, keepdims=True)
    sum_out[...] = jnp.broadcast_to(line, (SLABS, LANES))


in_vmem = pl.BlockSpec(memory_space=pltpu.VMEM)
in_smem = pl.BlockSpec(memory_space=pltpu.SMEM)
in_hbm = pl.BlockSpec(memory_space=pltpu.HBM)
table_scratch = pltpu.VMEM((2, 2 * N, 2 * N), jnp.bfloat16)


def f32(*shape):
    return jax.ShapeDtypeStruct(shape, jnp.float32)


def run(kernel, out_shape, in_specs, operands, scratch=(), mib=16):
    several = isinstance(out_shape, tuple)
    return pl.pallas_call(
        kernel,
        out_shape=out_shape,
        in_specs=in_specs,
        out_specs=(in_vmem,) * len(out_shape) if several else in_vmem,
        scratch_shapes=list(scratch),
        compiler_params=pltpu.CompilerParams(vmem_limit_bytes=mib << 20),
        name=kernel.__name__,
    )(*operands)


def passed_along(value, steps):
    pairs = [(source, (source + steps) % SLABS) for source in range(SLABS)]
    return lax.ppermute(value, "slab", pairs)


def body(lambdas, charge_a, charge_b, perturbed, grid_index, spline_weights, spline_slopes):
    slab = lax.axis_index("slab").reshape(1)
    inputs = (lambdas, charge_a, charge_b, perturbed, grid_index, spline_weights)
    own = run(
        pack_kernel,
        f32(8, WINDOWS, HERE),
        [in_smem] + [in_hbm] * 6,
        (slab, *inputs),
        [pltpu.SMEM((WINDOWS,), jnp.float32)]
        + [pltpu.VMEM(a.shape, a.dtype) for a in inputs[1:]]
        + [pltpu.SemaphoreType.DMA((6,))],
        mib=4,
    )
    below = passed_along(own, 1)
    far = passed_along(own, 2)
    kept = lambda count, rows: pltpu.VMEM((count, rows, WINDOWS, HERE), jnp.float32)
    from_own = run(
        own_spread_kernel, f32(WINDOWS, N, 2 * N), [in_vmem], (own,), [kept(1, 30)]
    )
    spectrum = run(
        spread_kernel,
        f32(2, N // 4, 2, 8, N),
        [in_vmem] * 3 + [in_hbm] * 2,
        (from_own, below, far, Y_FORWARD, X_FORWARD),
        [kept(2, 30), table_scratch, table_scratch, pltpu.SemaphoreType.DMA((2,))],
    )
    influence = run(influence_kernel, f32(N, 4 * N), [in_smem], (slab,), mib=4)
    columns = lax.all_to_all(spectrum.reshape(SLABS, 16, N), "slab", 0, 0, tiled=True)
    columns = run(
        column_kernel,
        f32(8 * N, N),
        [in_vmem] * 4,
        (columns.reshape(8 * N, N), influence, Z_FORWARD, Z_INVERSE),
        mib=8,
    )
    levels = lax.all_to_all(columns.reshape(SLABS, 16, N), "slab", 0, 0, tiled=True)
    part = f32(3, WINDOWS, HERE)
    mine, for_below, for_far, sums = run(
        sample_kernel,
        (part, part, part, f32(SLABS, N)),
        [in_vmem] * 6,
        (levels.reshape(2, N // 4, 2, 8, N), own, below, far, X_INVERSE, Y_INVERSE),
        [kept(3, 34), pltpu.VMEM((8, LANES), jnp.float32)],
    )
    from_above = passed_along(for_below, -1)
    from_far = passed_along(for_far, -2)
    sums = lax.all_to_all(sums.reshape(SLABS, 1, N), "slab", 0, 0, tiled=True)
    sums = jnp.sum(sums, axis=(0, 1))
    return (
        mine + from_above + from_far,
        sums[:WINDOWS] * (0.5 / ATOMS),
        sums[WINDOWS : 2 * WINDOWS] * (1.0 / ATOMS),
    )


def solution(mesh):
    return jax.shard_map(
        body,
        mesh=mesh,
        in_specs=(
            P("win"),
            P("win", "slab"),
            P("win", "slab"),
            P("win", "slab"),
            P(None, "win", "slab"),
            P(None, None, "win", "slab"),
            P(None, None, "win", "slab"),
        ),
        out_specs=(P(None, "win", "slab"), P("win"), P("win")),
        check_vma=False,
    )
```

time: 86.7 us -> 76.9 us (0.89)
  blocking collectives: 39.1 us -> 17 us
  waiting for transfers between devices: 12.2 us -> 27.2 us
  Pallas kernels: 21.2 us -> 11.2 us
  starting transfers between devices: 10.6 us -> 14.7 us
  local copies, waits for them, and re-layouts: 1.25 us -> 4.39 us
    all_to_all x1 -> x0, blocking collectives: 21 us -> none  [body(): lax.all_to_all(spectrum.reshape(SLABS, 16, N), 'slab', 0, 0, tiled=True)]
    all_to_all x0 -> x1, waiting for transfers between devices: none -> 12.7 us  [body(): lax.all_to_all(spectrum.reshape(SLABS, 16, N), 'slab', 0, 0, tiled=True)]
    pallas_call x4 -> x6, Pallas kernels: 21.2 us -> 11.2 us  [run(): pl.pallas_call(kernel, out_shape=out_shape, in_specs=in_specs, out_specs=...]
    all_to_all x0 -> x1, starting transfers between devices: none -> 4.46 us  [body(): lax.all_to_all(spectrum.reshape(SLABS, 16, N), 'slab', 0, 0, tiled=True)]
    unnamed x6 -> x20, local copies, waits for them, and re-layouts: 1.25 us -> 4.39 us
    ppermute x4, waiting for transfers between devices: 4.92 us -> 7.24 us  [passed_along(): return lax.ppermute(value, 'slab', pairs)]
    all_to_all x1, blocking collectives: 18.2 us -> 17 us  [body(): lax.all_to_all(columns.reshape(SLABS, 16, N), 'slab', 0, 0, tiled=True)]
  transfers between devices with their start and end apart: 5 -> 6, of which waited for: 2 -> 3; matrix products, arithmetic and copies ran while one was open for 1% -> 1% of each run, Pallas kernels for 0% -> 2%
where the time goes in v1:
time: 76.9 us; the launch traced here: 76.5 us
  waiting for transfers between devices  27.2 us (35%)
  blocking collectives  17 us (22%)
  starting transfers between devices  14.7 us (19%)
  Pallas kernels  11.2 us (15%)
  local copies, waits for them, and re-layouts  4.39 us (6%)
  other arithmetic  1.29 us (2%)
  between operations  0.77 us (1%)
    all_to_all x1, blocking collectives, body(): lax.all_to_all(columns.reshape(SLABS, 16, N), 'slab', 0, 0, tiled=True)  17 us
    all_to_all x1, waiting for transfers between devices, body(): lax.all_to_all(spectrum.reshape(SLABS, 16, N), 'slab', 0, 0, tiled=True)  12.7 us
    pallas_call x6, Pallas kernels, run(): pl.pallas_call(kernel, out_shape=out_shape, in_specs=in_specs, out_specs=...  11.2 us
    ppermute x4, waiting for transfers between devices, passed_along(): return lax.ppermute(value, 'slab', pairs)  7.24 us
    all_to_all x1, waiting for transfers between devices, body(): sums = lax.all_to_all(sums.reshape(SLABS, 1, N), 'slab', 0, 0, tiled=True)  7.18 us
    ppermute x4, starting transfers between devices, passed_along(): return lax.ppermute(value, 'slab', pairs)  5.19 us
    all_to_all x1, starting transfers between devices, body(): sums = lax.all_to_all(sums.reshape(SLABS, 1, N), 'slab', 0, 0, tiled=True)  5.05 us
    all_to_all x1, starting transfers between devices, body(): lax.all_to_all(spectrum.reshape(SLABS, 16, N), 'slab', 0, 0, tiled=True)  4.46 us
  transfers between devices with their start and end apart: 6, of which 3 were waited for; matrix products, arithmetic and copies ran while one was open for 1% of the time, Pallas kernels for 2%

profile of v1, /device:TPU:1, one launch (start us, length us, event | category | flops | bytes accessed | tf_op | source)
XLA Modules:
  0.0 76.5 jit_solution(17144839154026915072)
XLA Ops:
  0.6 0.0 copy-start.9
  0.6 0.6 copy-done.9
  1.3 0.0 copy-start.4
  1.3 0.9 %copy-done.4 = f32[3,4,4,512]{3,2,1,0:T(4,128)S(1)} copy-done((f32[3,4,4,512]{3,2,1,0:T(4,128)S(1)}, f32[3,4,4,512]{3,2,1,0:T(4,128)}, u32[]{:S(2)}) %copy-start.4) | copy-done | bytes 98328
  2.2 0.0 copy-start.5
  2.2 0.7 copy-done.5
  2.9 0.0 copy-start.6
  2.9 0.7 copy-done.6
  3.6 0.0 copy-start.7
  3.6 0.7 copy-done.7
  4.3 0.0 copy-start.8
  4.3 0.7 copy-done.8
  5.0 0.6 pack_kernel.1.own_ref
  5.6 0.0 copy-start.1
  5.6 0.0 copy-start.3
  5.7 3.1 %collective-permute-start = (f32[8,4,512]{2,1,0:T(4,128)S(1)}, f32[8,4,512]{2,1,0:T(4,128)S(1)}, u32[]{:S(2)}, u32[]{:S(2)}) collective-permute-start(f32[8,4,512]{2,1,0:T(4,128)S(1)} %pack_kernel.1.own_ref), channel_id=1, source_target_pairs={{0,1},{1,2},{2,3},{3,4},{4,5},{5,6},{6,7},{7,8},{8,9},{9,10},{10,1... | collective-permute-start | bytes 196616 | tf_op jit(solution)/shard_map/ppermute | solution.py:421
  8.8 0.8 collective-permute-start.1
  9.5 1.1 %own_spread_kernel.1.own_ref = f32[4,128,256]{2,1,0:T(8,128)S(1)} custom-call(f32[8,4,512]{2,1,0:T(4,128)S(1)} %pack_kernel.1.own_ref), custom_call_target="tpu_custom_call" | custom-call | tf_op jit(solution)/shard_map/own_spread_kernel/pallas_call | solution.py:408
  10.6 0.0 collective-permute-done.below_ref
  10.6 7.2 %collective-permute-done.1.far_ref = f32[8,4,512]{2,1,0:T(4,128)S(1)} collective-permute-done((f32[8,4,512]{2,1,0:T(4,128)S(1)}, f32[8,4,512]{2,1,0:T(4,128)S(1)}, u32[]{:S(2)}, u32[]{:S(2)}) %collective-permute-start.1) | collective-permute-done | bytes 65568 | tf_op jit(solution)/shard_map/ppermute | solution.py:421
  17.8 0.0 copy-done.1
  17.8 0.0 copy-done.3
  17.8 3.6 %spread_kernel.1 = f32[2,32,2,8,128]{4,3,2,1,0:T(8,128)} custom-call(f32[4,128,256]{2,1,0:T(8,128)S(1)} %own_spread_kernel.1.own_ref, f32[8,4,512]{2,1,0:T(4,128)S(1)} %collective-permute-done.below_ref, f32[8,4,512]{2,1,0:T(4,128)S(1)} %collective-permute-done.1.far_ref, bf16[2,256,256]{2,1,0:T(8,128)(2,1)S(1)} %copy-done.1, bf16[2,256,256]{2,1,0:T(8,128)(2,1)S(1)} %copy-done.3), custom_call_target="tpu_custom_call" | custom-call | tf_op jit(solution)/shard_map/spread_kernel/pallas_call | solution.py:408
  21.5 4.5 %all-to-all-start = ((f32[64,16,128]{2,1,0:T(8,128)}), f32[64,16,128]{2,1,0:T(8,128)S(1)}, u32[]{:S(2)}, u32[]{:S(2)}) async-start(f32[64,16,128]{2,1,0:T(8,128)} %bitcast.1), calls=%async_computation | async-start | bytes 1048576 | tf_op jit(solution)/shard_map/all_to_all | solution.py:451
  25.9 0.0 copy-start
  25.9 0.1 influence_kernel.1.influence_ref
  26.1 12.7 %all-to-all-done = f32[64,16,128]{2,1,0:T(8,128)S(1)} async-done(((f32[64,16,128]{2,1,0:T(8,128)}), f32[64,16,128]{2,1,0:T(8,128)S(1)}, u32[]{:S(2)}, u32[]{:S(2)}) %all-to-all-start) | async-done | bytes 524320 | tf_op jit(solution)/shard_map/all_to_all | solution.py:451
  38.8 0.0 copy-done
  38.8 0.8 %column_kernel.1 = f32[1024,128]{1,0:T(8,128)S(1)} custom-call(f32[1024,128]{1,0:T(8,128)S(1)} %bitcast.8, f32[128,512]{1,0:T(8,128)S(1)} %influence_kernel.1.influence_ref, bf16[2,256,256]{2,1,0:T(8,128)(2,1)S(1)} %copy-done, bf16[2,256,256]{2,1,0:T(8,128)(2,1)S(1)} %copy-done.1), custom_call_target="tpu_custom_call" | custom-call | tf_op jit(solution)/shard_map/column_kernel/pallas_call | solution.py:408
  39.6 0.0 copy-start.2
  39.7 17.0 %all_to_all.15 = f32[64,16,128]{2,1,0:T(8,128)S(1)} all-to-all(f32[64,16,128]{2,1,0:T(8,128)S(1)} %bitcast.9), channel_id=1, replica_groups=mesh['win'=4,'slab'=64] {'slab'}, dimensions={0} | all-to-all | bytes 1048576 | tf_op jit(solution)/shard_map/all_to_all | solution.py:459
  56.7 0.0 copy-done.2
  56.7 4.9 %sample_kernel.1 = (f32[3,4,512]{2,1,0:T(4,128)S(1)}, f32[3,4,512]{2,1,0:T(4,128)S(1)}, f32[3,4,512]{2,1,0:T(4,128)S(1)}, f32[64,128]{1,0:T(8,128)}) custom-call(f32[2,32,2,8,128]{4,3,2,1,0:T(8,128)S(1)} %bitcast.10, f32[8,4,512]{2,1,0:T(4,128)S(1)} %pack_kernel.1.own_ref, f32[8,4,512]{2,1,0:T(4,128)S(1)} %collective-permute-done.below_ref, ...), custom_call_target="tpu_custom_call" | custom-call | tf_op jit(solution)/shard_map/sample_kernel/pallas_call | solution.py:408
  61.6 0.5 collective-permute-start.2
  62.0 0.9 %collective-permute-start.3 = (f32[3,4,512]{2,1,0:T(4,128)S(1)}, f32[3,4,512]{2,1,0:T(4,128)S(1)}, u32[]{:S(2)}, u32[]{:S(2)}) collective-permute-start(f32[3,4,512]{2,1,0:T(4,128)S(1)} %get-tuple-element.9), channel_id=1, source_target_pairs={{0,62},{1,63},{2,0},{3,1},{4,2},{5,3},{6,4},{7,5},{8,6},{9,7},{10,... | collective-permute-start | bytes 73736 | tf_op jit(solution)/shard_map/ppermute | solution.py:421
  62.9 5.0 %all-to-all-start.2 = ((f32[64,1,128]{2,1,0:T(1,128)}), f32[64,1,128]{2,1,0:T(1,128)S(1)}, u32[]{:S(2)}, u32[]{:S(2)}) async-start(f32[64,1,128]{2,1,0:T(1,128)} %bitcast.6), calls=%async_computation.2 | async-start | bytes 65536 | tf_op jit(solution)/shard_map/all_to_all | solution.py:470
  68.0 0.0 collective-permute-done.2
  68.0 0.0 collective-permute-done.3
  68.0 0.6 add_add_fusion
  68.6 7.2 %all-to-all-done.2 = f32[64,1,128]{2,1,0:T(1,128)S(1)} async-done(((f32[64,1,128]{2,1,0:T(1,128)}), f32[64,1,128]{2,1,0:T(1,128)S(1)}, u32[]{:S(2)}, u32[]{:S(2)}) %all-to-all-start.2) | async-done | bytes 32800 | tf_op jit(solution)/shard_map/all_to_all | solution.py:470
  75.8 0.1 reduce_sum.9
  75.9 0.6 slice_multiply_fusion
Async XLA Ops:
  0.6 0.7 copy-start.9
  1.3 0.9 %copy-start.4 = (f32[3,4,4,512]{3,2,1,0:T(4,128)S(1)}, f32[3,4,4,512]{3,2,1,0:T(4,128)}, u32[]{:S(2)}) copy-start(f32[3,4,4,512]{3,2,1,0:T(4,128)} %refs_5_.1) | copy-start | bytes 294916
  2.2 0.7 copy-start.5
  2.9 0.7 copy-start.6
  3.6 0.7 copy-start.7
  4.3 0.7 copy-start.8
  5.6 12.2 %copy-start.1 = (bf16[2,256,256]{2,1,0:T(8,128)(2,1)S(1)}, bf16[2,256,256]{2,1,0:T(8,128)(2,1)}, u32[]{:S(2)}) copy-start(bf16[2,256,256]{2,1,0:T(8,128)(2,1)} %constant.18.clone.y_hbm.inverse_ref) | copy-start | bytes 786436
  5.6 12.2 %copy-start.3 = (bf16[2,256,256]{2,1,0:T(8,128)(2,1)S(1)}, bf16[2,256,256]{2,1,0:T(8,128)(2,1)}, u32[]{:S(2)}) copy-start(bf16[2,256,256]{2,1,0:T(8,128)(2,1)} %constant.19.clone.x_hbm) | copy-start | bytes 786436
  5.7 4.9 %collective-permute-start = (f32[8,4,512]{2,1,0:T(4,128)S(1)}, f32[8,4,512]{2,1,0:T(4,128)S(1)}, u32[]{:S(2)}, u32[]{:S(2)}) collective-permute-start(f32[8,4,512]{2,1,0:T(4,128)S(1)} %pack_kernel.1.own_ref), channel_id=1, source_target_pairs={{0,1},{1,2},{2,3},{3,4},{4,5},{5,6},{6,7},{7,8},{8,9},{9,10},{10,1... | collective-permute-start | bytes 196616 | tf_op jit(solution)/shard_map/ppermute | solution.py:421
  8.8 9.1 %collective-permute-start.1 = (f32[8,4,512]{2,1,0:T(4,128)S(1)}, f32[8,4,512]{2,1,0:T(4,128)S(1)}, u32[]{:S(2)}, u32[]{:S(2)}) collective-permute-start(f32[8,4,512]{2,1,0:T(4,128)S(1)} %pack_kernel.1.own_ref), channel_id=1, source_target_pairs={{0,2},{1,3},{2,4},{3,5},{4,6},{5,7},{6,8},{7,9},{8,10},{9,11},{10,... | collective-permute-start | bytes 196616 | tf_op jit(solution)/shard_map/ppermute | solution.py:421
  21.5 17.3 %all-to-all-start = ((f32[64,16,128]{2,1,0:T(8,128)}), f32[64,16,128]{2,1,0:T(8,128)S(1)}, u32[]{:S(2)}, u32[]{:S(2)}) async-start(f32[64,16,128]{2,1,0:T(8,128)} %bitcast.1), calls=%async_computation | async-start | bytes 1048576 | tf_op jit(solution)/shard_map/all_to_all | solution.py:451
  25.9 12.9 %copy-start = (bf16[2,256,256]{2,1,0:T(8,128)(2,1)S(1)}, bf16[2,256,256]{2,1,0:T(8,128)(2,1)}, u32[]{:S(2)}) copy-start(bf16[2,256,256]{2,1,0:T(8,128)(2,1)} %constant.20.clone.forward_ref.y_ref) | copy-start | bytes 786436
  39.6 17.0 %copy-start.2 = (bf16[2,256,256]{2,1,0:T(8,128)(2,1)S(1)}, bf16[2,256,256]{2,1,0:T(8,128)(2,1)}, u32[]{:S(2)}) copy-start(bf16[2,256,256]{2,1,0:T(8,128)(2,1)} %constant.21.clone.x_ref) | copy-start | bytes 786436
  61.6 6.4 %collective-permute-start.2 = (f32[3,4,512]{2,1,0:T(4,128)S(1)}, f32[3,4,512]{2,1,0:T(4,128)S(1)}, u32[]{:S(2)}, u32[]{:S(2)}) collective-permute-start(f32[3,4,512]{2,1,0:T(4,128)S(1)} %get-tuple-element.8), channel_id=1, source_target_pairs={{0,63},{1,0},{2,1},{3,2},{4,3},{5,4},{6,5},{7,6},{8,7},{9,8},{10,9... | collective-permute-start | bytes 73736 | tf_op jit(solution)/shard_map/ppermute | solution.py:421
  62.0 5.9 %collective-permute-start.3 = (f32[3,4,512]{2,1,0:T(4,128)S(1)}, f32[3,4,512]{2,1,0:T(4,128)S(1)}, u32[]{:S(2)}, u32[]{:S(2)}) collective-permute-start(f32[3,4,512]{2,1,0:T(4,128)S(1)} %get-tuple-element.9), channel_id=1, source_target_pairs={{0,62},{1,63},{2,0},{3,1},{4,2},{5,3},{6,4},{7,5},{8,6},{9,7},{10,... | collective-permute-start | bytes 73736 | tf_op jit(solution)/shard_map/ppermute | solution.py:421
  62.9 12.9 %all-to-all-start.2 = ((f32[64,1,128]{2,1,0:T(1,128)}), f32[64,1,128]{2,1,0:T(1,128)S(1)}, u32[]{:S(2)}, u32[]{:S(2)}) async-start(f32[64,1,128]{2,1,0:T(1,128)} %bitcast.6), calls=%async_computation.2 | async-start | bytes 65536 | tf_op jit(solution)/shard_map/all_to_all | solution.py:470

commit v2 on v1

--- a/solution.py
+++ b/solution.py
@@ -214,7 +214,8 @@
     return planes
 
 
-def own_spread_kernel(own_ref, out_ref, keep):
+def own_spread_kernel(slab_ref, own_ref, out_ref, influence_ref, keep):
+    fill_influence(slab_ref, influence_ref)
     for w, planes in enumerate(spread_planes(((0, own_ref),), keep)):
         out_ref[w] = planes
 
@@ -255,7 +256,7 @@
     return jnp.where(counter >= N // 2, counter - N, counter).astype(jnp.float32) / N
 
 
-def influence_kernel(slab_ref, out_ref):
+def fill_influence(slab_ref, out_ref):
     first = lax.rem(slab_ref[0], SLABS // 2) * 4
     shape = (N, N)
     freq_z = frequency(lax.broadcasted_iota(jnp.int32, shape, 0))
@@ -393,6 +394,15 @@
     sum_out[...] = jnp.broadcast_to(line, (SLABS, LANES))
 
 
+def finish_kernel(mine_ref, above_ref, far_ref, sum_ref, force_out, energy_out, slope_out):
+    force_out[...] = mine_ref[...] + above_ref[...] + far_ref[...]
+    line = jnp.sum(sum_ref[...], axis=0, keepdims=True)
+    lane = lax.broadcasted_iota(jnp.int32, (1, LANES), 1)
+    for w in range(WINDOWS):
+        energy_out[w] = jnp.sum(jnp.where(lane == w, line, 0.0)) * (0.5 / ATOMS)
+        slope_out[w] = jnp.sum(jnp.where(lane == WINDOWS + w, line, 0.0)) * (1.0 / ATOMS)
+
+
 in_vmem = pl.BlockSpec(memory_space=pltpu.VMEM)
 in_smem = pl.BlockSpec(memory_space=pltpu.SMEM)
 in_hbm = pl.BlockSpec(memory_space=pltpu.HBM)
@@ -432,13 +442,17 @@
         [pltpu.SMEM((WINDOWS,), jnp.float32)]
         + [pltpu.VMEM(a.shape, a.dtype) for a in inputs[1:]]
         + [pltpu.SemaphoreType.DMA((6,))],
-        mib=4,
+        mib=60,
     )
     below = passed_along(own, 1)
     far = passed_along(own, 2)
     kept = lambda count, rows: pltpu.VMEM((count, rows, WINDOWS, HERE), jnp.float32)
-    from_own = run(
-        own_spread_kernel, f32(WINDOWS, N, 2 * N), [in_vmem], (own,), [kept(1, 30)]
+    from_own, influence = run(
+        own_spread_kernel,
+        (f32(WINDOWS, N, 2 * N), f32(N, 4 * N)),
+        [in_smem, in_vmem],
+        (slab, own),
+        [kept(1, 30)],
     )
     spectrum = run(
         spread_kernel,
@@ -447,7 +461,6 @@
         (from_own, below, far, Y_FORWARD, X_FORWARD),
         [kept(2, 30), table_scratch, table_scratch, pltpu.SemaphoreType.DMA((2,))],
     )
-    influence = run(influence_kernel, f32(N, 4 * N), [in_smem], (slab,), mib=4)
     columns = lax.all_to_all(spectrum.reshape(SLABS, 16, N), "slab", 0, 0, tiled=True)
     columns = run(
         column_kernel,
@@ -468,12 +481,14 @@
     from_above = passed_along(for_below, -1)
     from_far = passed_along(for_far, -2)
     sums = lax.all_to_all(sums.reshape(SLABS, 1, N), "slab", 0, 0, tiled=True)
-    sums = jnp.sum(sums, axis=(0, 1))
-    return (
-        mine + from_above + from_far,
-        sums[:WINDOWS] * (0.5 / ATOMS),
-        sums[WINDOWS : 2 * WINDOWS] * (1.0 / ATOMS),
-    )
+    return pl.pallas_call(
+        finish_kernel,
+        out_shape=(part, f32(WINDOWS), f32(WINDOWS)),
+        in_specs=[in_vmem] * 4,
+        out_specs=(in_vmem, in_smem, in_smem),
+        compiler_params=pltpu.CompilerParams(vmem_limit_bytes=4 << 20),
+        name="finish_kernel",
+    )(mine, from_above, from_far, sums.reshape(SLABS, N))
 
 
 def solution(mesh):

time: 76.9 us -> 71.6 us (0.931)
  waiting for transfers between devices: 27.2 us -> 4.27 us
  blocking collectives: 17 us -> 36.5 us
  local copies, waits for them, and re-layouts: 4.39 us -> 1.85 us
  other arithmetic: 1.29 us -> 0 us
  Pallas kernels: 11.2 us -> 12.1 us
    all_to_all x0 -> x1, blocking collectives: none -> 19.5 us  [body(): lax.all_to_all(spectrum.reshape(SLABS, 16, N), 'slab', 0, 0, tiled=True)]
    all_to_all x1 -> x0, waiting for transfers between devices: 12.7 us -> none  [body(): lax.all_to_all(spectrum.reshape(SLABS, 16, N), 'slab', 0, 0, tiled=True)]
    all_to_all x1, waiting for transfers between devices: 7.18 us -> 0.46 us  [body(): sums = lax.all_to_all(sums.reshape(SLABS, 1, N), 'slab', 0, 0, tiled=True)]
    ppermute x4, starting transfers between devices: 5.19 us -> 10.6 us  [passed_along(): return lax.ppermute(value, 'slab', pairs)]
    all_to_all x1 -> x0, starting transfers between devices: 4.46 us -> none  [body(): lax.all_to_all(spectrum.reshape(SLABS, 16, N), 'slab', 0, 0, tiled=True)]
    ppermute x4, waiting for transfers between devices: 7.24 us -> 3.81 us  [passed_along(): return lax.ppermute(value, 'slab', pairs)]
    unnamed x20 -> x12, local copies, waits for them, and re-layouts: 4.39 us -> 1.85 us
    pallas_call x6 -> x5, Pallas kernels: 11.2 us -> 11.4 us  [run(): pl.pallas_call(kernel, out_shape=out_shape, in_specs=in_specs, out_specs=...]
  transfers between devices with their start and end apart: 6 -> 5, of which waited for: 3 -> 3; matrix products, arithmetic and copies ran while one was open for 1% -> 0% of each run, Pallas kernels for 2% -> 2%
where the time goes in v2:
time: 71.6 us; the launch traced here: 70.5 us
  blocking collectives  36.5 us (51%)
  starting transfers between devices  15 us (21%)
  Pallas kernels  12.1 us (17%)
  waiting for transfers between devices  4.27 us (6%)
  local copies, waits for them, and re-layouts  1.85 us (3%)
  between operations  0.72 us (1%)
    all_to_all x1, blocking collectives, body(): lax.all_to_all(spectrum.reshape(SLABS, 16, N), 'slab', 0, 0, tiled=True)  19.5 us
    all_to_all x1, blocking collectives, body(): lax.all_to_all(columns.reshape(SLABS, 16, N), 'slab', 0, 0, tiled=True)  17 us
    pallas_call x5, Pallas kernels, run(): pl.pallas_call(kernel, out_shape=out_shape, in_specs=in_specs, out_specs=...  11.4 us
    ppermute x4, starting transfers between devices, passed_along(): return lax.ppermute(value, 'slab', pairs)  10.6 us
    all_to_all x1, starting transfers between devices, body(): sums = lax.all_to_all(sums.reshape(SLABS, 1, N), 'slab', 0, 0, tiled=True)  4.44 us
    ppermute x4, waiting for transfers between devices, passed_along(): return lax.ppermute(value, 'slab', pairs)  3.81 us
    unnamed x12, local copies, waits for them, and re-layouts  1.85 us
  transfers between devices with their start and end apart: 5, of which 3 were waited for; matrix products, arithmetic and copies ran while one was open for 0% of the time, Pallas kernels for 2%

profile of v2, /device:TPU:1, one launch (start us, length us, event | category | flops | bytes accessed | tf_op | source)
XLA Modules:
  0.0 70.5 jit_solution(7867159621844942697)
XLA Ops:
  0.6 0.0 copy-start.1
  0.6 1.7 %pack_kernel.1.own_ref = f32[8,4,512]{2,1,0:T(4,128)} custom-call(s32[1]{0:T(128)} %bitcast.slab_ref, f32[4]{0:T(128)} %refs_0_.1, f32[4,512]{1,0:T(4,128)} %refs_1_.1, f32[4,512]{1,0:T(4,128)} %refs_2_.1, s32[4,512]{1,0:T(4,128)} %refs_3_.1, s32[3,4,512]{2,1,0:T(4,128)} %refs_4_.1, f32[3,4,4,512]{3,2,1,0:T(4,128)} %refs_5_.1), custom_call_target="tpu_custom_call" | custom-call | tf_op jit(solution)/shard_map/pack_kernel/pallas_call | solution.py:418
  2.3 2.5 %collective-permute-start.1 = (f32[8,4,512]{2,1,0:T(4,128)}, f32[8,4,512]{2,1,0:T(4,128)S(1)}, u32[]{:S(2)}, u32[]{:S(2)}) collective-permute-start(f32[8,4,512]{2,1,0:T(4,128)} %pack_kernel.1.own_ref), channel_id=1, source_target_pairs={{0,2},{1,3},{2,4},{3,5},{4,6},{5,7},{6,8},{7,9},{8,10},{9,11},{10,... | collective-permute-start | bytes 196616 | tf_op jit(solution)/shard_map/ppermute | solution.py:431
  4.9 1.6 %collective-permute-start = (f32[8,4,512]{2,1,0:T(4,128)}, f32[8,4,512]{2,1,0:T(4,128)S(1)}, u32[]{:S(2)}, u32[]{:S(2)}) collective-permute-start(f32[8,4,512]{2,1,0:T(4,128)} %pack_kernel.1.own_ref), channel_id=1, source_target_pairs={{0,1},{1,2},{2,3},{3,4},{4,5},{5,6},{6,7},{7,8},{8,9},{9,10},{10,1... | collective-permute-start | bytes 196616 | tf_op jit(solution)/shard_map/ppermute | solution.py:431
  6.5 0.0 copy-start.2
  6.5 0.9 %copy-done.2 = f32[8,4,512]{2,1,0:T(4,128)S(1)} copy-done((f32[8,4,512]{2,1,0:T(4,128)S(1)}, f32[8,4,512]{2,1,0:T(4,128)}, u32[]{:S(2)}) %copy-start.2) | copy-done | bytes 65560
  7.3 1.2 %own_spread_kernel.1 = (f32[4,128,256]{2,1,0:T(8,128)S(1)}, f32[128,512]{1,0:T(8,128)S(1)}) custom-call(s32[1]{0:T(128)} %bitcast.slab_ref, f32[8,4,512]{2,1,0:T(4,128)S(1)} %copy-done.2), custom_call_target="tpu_custom_call" | custom-call | tf_op jit(solution)/shard_map/own_spread_kernel/pallas_call | solution.py:418
  8.5 2.9 %collective-permute-done.1.far_ref = f32[8,4,512]{2,1,0:T(4,128)S(1)} collective-permute-done((f32[8,4,512]{2,1,0:T(4,128)}, f32[8,4,512]{2,1,0:T(4,128)S(1)}, u32[]{:S(2)}, u32[]{:S(2)}) %collective-permute-start.1) | collective-permute-done | bytes 65568 | tf_op jit(solution)/shard_map/ppermute | solution.py:431
  11.4 0.0 collective-permute-done.below_ref
  11.4 0.0 copy-done.1
  11.4 0.0 copy-start.5
  11.4 0.9 %copy-done.5 = bf16[2,256,256]{2,1,0:T(8,128)(2,1)S(1)} copy-done((bf16[2,256,256]{2,1,0:T(8,128)(2,1)S(1)}, bf16[2,256,256]{2,1,0:T(8,128)(2,1)}, u32[]{:S(2)}) %copy-start.5) | copy-done | bytes 262168
  12.3 2.8 %spread_kernel.1 = f32[2,32,2,8,128]{4,3,2,1,0:T(8,128)S(1)} custom-call(f32[4,128,256]{2,1,0:T(8,128)S(1)} %get-tuple-element.9.own_ref, f32[8,4,512]{2,1,0:T(4,128)S(1)} %collective-permute-done.below_ref, f32[8,4,512]{2,1,0:T(4,128)S(1)} %collective-permute-done.1.far_ref, bf16[2,256,256]{2,1,0:T(8,128)(2,1)S(1)} %copy-done.1, ...), custom_call_target="tpu_custom_call" | custom-call | tf_op jit(solution)/shard_map/spread_kernel/pallas_call | solution.py:418
  15.2 0.0 copy-start
  15.2 19.5 %all_to_all.15 = f32[64,16,128]{2,1,0:T(8,128)S(1)} all-to-all(f32[64,16,128]{2,1,0:T(8,128)S(1)} %bitcast.12), channel_id=1, replica_groups=mesh['win'=4,'slab'=64] {'slab'}, dimensions={0} | all-to-all | bytes 1048576 | tf_op jit(solution)/shard_map/all_to_all | solution.py:464
  34.7 0.0 copy-done
  34.7 0.8 %column_kernel.1 = f32[1024,128]{1,0:T(8,128)S(1)} custom-call(f32[1024,128]{1,0:T(8,128)S(1)} %bitcast.9, f32[128,512]{1,0:T(8,128)S(1)} %get-tuple-element.10.influence_ref, bf16[2,256,256]{2,1,0:T(8,128)(2,1)S(1)} %copy-done, bf16[2,256,256]{2,1,0:T(8,128)(2,1)S(1)} %copy-done.1), custom_call_target="tpu_custom_call" | custom-call | tf_op jit(solution)/shard_map/column_kernel/pallas_call | solution.py:418
  35.5 0.0 copy-start.3
  35.6 0.0 copy-start.4
  35.6 17.0 %all_to_all.16 = f32[64,16,128]{2,1,0:T(8,128)S(1)} all-to-all(f32[64,16,128]{2,1,0:T(8,128)S(1)} %bitcast.10), channel_id=1, replica_groups=mesh['win'=4,'slab'=64] {'slab'}, dimensions={0} | all-to-all | bytes 1048576 | tf_op jit(solution)/shard_map/all_to_all | solution.py:472
  52.6 0.0 copy-done.3
  52.6 0.0 copy-done.4
  52.6 4.9 %sample_kernel.1 = (f32[3,4,512]{2,1,0:T(4,128)S(1)}, f32[3,4,512]{2,1,0:T(4,128)S(1)}, f32[3,4,512]{2,1,0:T(4,128)S(1)}, f32[64,128]{1,0:T(8,128)}) custom-call(f32[2,32,2,8,128]{4,3,2,1,0:T(8,128)S(1)} %bitcast.11, f32[8,4,512]{2,1,0:T(4,128)S(1)} %copy-done.3, f32[8,4,512]{2,1,0:T(4,128)S(1)} %collective-permute-done.below_ref, ...), custom_call_target="tpu_custom_call" | custom-call | tf_op jit(solution)/shard_map/sample_kernel/pallas_call | solution.py:418
  57.5 4.4 %all-to-all-start.2 = ((f32[64,1,128]{2,1,0:T(1,128)}), f32[64,1,128]{2,1,0:T(1,128)S(1)}, u32[]{:S(2)}, u32[]{:S(2)}) async-start(f32[64,1,128]{2,1,0:T(1,128)} %bitcast.6), calls=%async_computation.2 | async-start | bytes 65536 | tf_op jit(solution)/shard_map/all_to_all | solution.py:483
  61.9 0.6 collective-permute-start.2
  62.6 5.8 %collective-permute-start.3 = (f32[3,4,512]{2,1,0:T(4,128)S(1)}, f32[3,4,512]{2,1,0:T(4,128)S(1)}, u32[]{:S(2)}, u32[]{:S(2)}) collective-permute-start(f32[3,4,512]{2,1,0:T(4,128)S(1)} %get-tuple-element.13), channel_id=1, source_target_pairs={{0,62},{1,63},{2,0},{3,1},{4,2},{5,3},{6,4},{7,5},{8,6},{9,7},{10,... | collective-permute-start | bytes 73736 | tf_op jit(solution)/shard_map/ppermute | solution.py:431
  68.4 0.0 collective-permute-done.2.above_ref
  68.4 0.9 %collective-permute-done.3.far_ref = f32[3,4,512]{2,1,0:T(4,128)S(1)} collective-permute-done((f32[3,4,512]{2,1,0:T(4,128)S(1)}, f32[3,4,512]{2,1,0:T(4,128)S(1)}, u32[]{:S(2)}, u32[]{:S(2)}) %collective-permute-start.3) | collective-permute-done | bytes 24608 | tf_op jit(solution)/shard_map/ppermute | solution.py:431
  69.4 0.5 all-to-all-done.2
  69.8 0.7 finish_kernel.1
Async XLA Ops:
  0.6 10.8 %copy-start.1 = (bf16[2,256,256]{2,1,0:T(8,128)(2,1)S(1)}, bf16[2,256,256]{2,1,0:T(8,128)(2,1)}, u32[]{:S(2)}) copy-start(bf16[2,256,256]{2,1,0:T(8,128)(2,1)} %constant.12.clone.y_hbm.inverse_ref) | copy-start | bytes 786436
  2.3 9.0 %collective-permute-start.1 = (f32[8,4,512]{2,1,0:T(4,128)}, f32[8,4,512]{2,1,0:T(4,128)S(1)}, u32[]{:S(2)}, u32[]{:S(2)}) collective-permute-start(f32[8,4,512]{2,1,0:T(4,128)} %pack_kernel.1.own_ref), channel_id=1, source_target_pairs={{0,2},{1,3},{2,4},{3,5},{4,6},{5,7},{6,8},{7,9},{8,10},{9,11},{10,... | collective-permute-start | bytes 196616 | tf_op jit(solution)/shard_map/ppermute | solution.py:431
  4.9 6.5 %collective-permute-start = (f32[8,4,512]{2,1,0:T(4,128)}, f32[8,4,512]{2,1,0:T(4,128)S(1)}, u32[]{:S(2)}, u32[]{:S(2)}) collective-permute-start(f32[8,4,512]{2,1,0:T(4,128)} %pack_kernel.1.own_ref), channel_id=1, source_target_pairs={{0,1},{1,2},{2,3},{3,4},{4,5},{5,6},{6,7},{7,8},{8,9},{9,10},{10,1... | collective-permute-start | bytes 196616 | tf_op jit(solution)/shard_map/ppermute | solution.py:431
  6.5 0.9 %copy-start.2 = (f32[8,4,512]{2,1,0:T(4,128)S(1)}, f32[8,4,512]{2,1,0:T(4,128)}, u32[]{:S(2)}) copy-start(f32[8,4,512]{2,1,0:T(4,128)} %pack_kernel.1.own_ref) | copy-start | bytes 196612
  11.4 1.0 %copy-start.5 = (bf16[2,256,256]{2,1,0:T(8,128)(2,1)S(1)}, bf16[2,256,256]{2,1,0:T(8,128)(2,1)}, u32[]{:S(2)}) copy-start(bf16[2,256,256]{2,1,0:T(8,128)(2,1)} %constant.13.clone.x_hbm) | copy-start | bytes 786436
  15.2 19.5 %copy-start = (bf16[2,256,256]{2,1,0:T(8,128)(2,1)S(1)}, bf16[2,256,256]{2,1,0:T(8,128)(2,1)}, u32[]{:S(2)}) copy-start(bf16[2,256,256]{2,1,0:T(8,128)(2,1)} %constant.14.clone.forward_ref.y_ref) | copy-start | bytes 786436
  35.5 17.0 %copy-start.3 = (f32[8,4,512]{2,1,0:T(4,128)S(1)}, f32[8,4,512]{2,1,0:T(4,128)}, u32[]{:S(2)}) copy-start(f32[8,4,512]{2,1,0:T(4,128)} %pack_kernel.1.own_ref) | copy-start | bytes 196612
  35.6 17.0 %copy-start.4 = (bf16[2,256,256]{2,1,0:T(8,128)(2,1)S(1)}, bf16[2,256,256]{2,1,0:T(8,128)(2,1)}, u32[]{:S(2)}) copy-start(bf16[2,256,256]{2,1,0:T(8,128)(2,1)} %constant.15.clone.x_ref) | copy-start | bytes 786436
  57.5 12.3 %all-to-all-start.2 = ((f32[64,1,128]{2,1,0:T(1,128)}), f32[64,1,128]{2,1,0:T(1,128)S(1)}, u32[]{:S(2)}, u32[]{:S(2)}) async-start(f32[64,1,128]{2,1,0:T(1,128)} %bitcast.6), calls=%async_computation.2 | async-start | bytes 65536 | tf_op jit(solution)/shard_map/all_to_all | solution.py:483
  61.9 6.5 %collective-permute-start.2 = (f32[3,4,512]{2,1,0:T(4,128)S(1)}, f32[3,4,512]{2,1,0:T(4,128)S(1)}, u32[]{:S(2)}, u32[]{:S(2)}) collective-permute-start(f32[3,4,512]{2,1,0:T(4,128)S(1)} %get-tuple-element.12), channel_id=1, source_target_pairs={{0,63},{1,0},{2,1},{3,2},{4,3},{5,4},{6,5},{7,6},{8,7},{9,8},{10,9... | collective-permute-start | bytes 73736 | tf_op jit(solution)/shard_map/ppermute | solution.py:431
  62.6 6.8 %collective-permute-start.3 = (f32[3,4,512]{2,1,0:T(4,128)S(1)}, f32[3,4,512]{2,1,0:T(4,128)S(1)}, u32[]{:S(2)}, u32[]{:S(2)}) collective-permute-start(f32[3,4,512]{2,1,0:T(4,128)S(1)} %get-tuple-element.13), channel_id=1, source_target_pairs={{0,62},{1,63},{2,0},{3,1},{4,2},{5,3},{6,4},{7,5},{8,6},{9,7},{10,... | collective-permute-start | bytes 73736 | tf_op jit(solution)/shard_map/ppermute | solution.py:431

commit v3 on v2

v3 whole, which is shorter than its diff:
```python
import math

import jax
import jax.numpy as jnp
import numpy as np
from jax import lax
from jax.experimental import pallas as pl
from jax.experimental.pallas import tpu as pltpu
from jax.sharding import PartitionSpec as P

N = 128
LANES = 128
WINDOWS = 4
HERE = 512
SLABS = 64
CHIPS = SLABS // 2
PAIR = WINDOWS // 2
DEEP = 4
ATOMS = SLABS * HERE
gauss_width = 2.0


def blocks(real, imaginary):
    return np.block([[real, -imaginary], [imaginary, real]])


def tables():
    k = np.arange(N)
    angle = 2.0 * np.pi * ((k[:, None] * k[None, :]) % N) / N
    cosine, sine = np.cos(angle), np.sin(angle)
    forward = blocks(cosine, -sine)
    inverse = blocks(cosine, sine)
    order = np.arange(2 * N).reshape(2, N // 4, 4).transpose(1, 0, 2).ravel()
    return tuple(
        np.ascontiguousarray(m, dtype=np.float32)
        for m in (
            forward.T,
            forward[order],
            forward,
            inverse,
            inverse[:, order],
            inverse.T,
        )
    )


def halves(x):
    top = x.astype(jnp.bfloat16)
    return top, (x - top.astype(jnp.float32)).astype(jnp.bfloat16)


def table_halves(table):
    top = table.astype(jnp.bfloat16)
    return np.stack([top, (table - top.astype(np.float32)).astype(jnp.bfloat16)])


Y_FORWARD, X_FORWARD, Z_FORWARD, Z_INVERSE, X_INVERSE, Y_INVERSE = map(table_halves, tables())


def dot(a, b, contract=(1, 0)):
    dims = (((contract[0],), (contract[1],)), ((), ()))
    return lax.dot_general(a, b, dims, preferred_element_type=jnp.float32)


def table_times(table_ref, x):
    top, rest = halves(x)
    return dot(table_ref[0], top) + dot(table_ref[1], top) + dot(table_ref[0], rest)


def times_table(x, table_ref):
    top, rest = halves(x)
    return dot(top, table_ref[0]) + dot(rest, table_ref[0]) + dot(top, table_ref[1])


def weights_of(u):
    v = 1.0 - u
    return (
        v * v * v * (1.0 / 6.0),
        (0.5 * u - 1.0) * u * u + (2.0 / 3.0),
        (0.5 * v - 1.0) * v * v + (2.0 / 3.0),
        u * u * u * (1.0 / 6.0),
    )


def slopes_of(u):
    v = 1.0 - u
    return (-0.5 * v * v, (1.5 * u - 2.0) * u, (2.0 - 1.5 * v) * v, 0.5 * u * u)


def pack_kernel(slab_ref, *refs):
    sources, (mine_ref, other_ref), landed, sem = refs[:6], refs[6:8], refs[8:14], refs[14]
    copies = [
        pltpu.make_async_copy(source, target, sem.at[i])
        for i, (source, target) in enumerate(zip(sources, landed))
    ]
    for copy in copies:
        copy.start()
    for copy in copies:
        copy.wait()
    lambda_ref, a_ref, b_ref, flag_ref, index_ref, weight_ref = landed
    flags = flag_ref[...].astype(jnp.float32)
    steps = flags * (b_ref[...] - a_ref[...])
    core = lax.rem(slab_ref[0], 2)
    first = (slab_ref[0] - core) * 2
    row = lax.broadcasted_iota(jnp.int32, (WINDOWS, HERE), 0)
    scale = jnp.zeros((WINDOWS, HERE), jnp.float32)
    for w in range(WINDOWS):
        scale = jnp.where(row == w, lambda_ref[w], scale)
    values = [
        index_ref[0].astype(jnp.float32),
        index_ref[1].astype(jnp.float32),
        (index_ref[2] - first).astype(jnp.float32),
    ]
    for axis in range(3):
        values.append(weight_ref[axis, 2] + 2.0 * weight_ref[axis, 3] - weight_ref[axis, 0])
    values += [a_ref[...] + scale * steps, steps]
    for r, value in enumerate(values):
        lower, upper = value[:PAIR], value[PAIR:]
        mine_ref[r] = jnp.where(core == 0, lower, upper)
        other_ref[r] = jnp.where(core == 0, upper, lower)


def places(first, height):
    block = jnp.floor(first * (1.0 / height))
    after = jnp.where(block == float(N // height - 1), 0.0, block + 1.0)
    return block, after, first - height * block


def row_halves(value):
    top = value.astype(jnp.bfloat16).astype(jnp.float32)
    return top, value - top


def wide(row):
    return jnp.broadcast_to(row, (16, LANES)).astype(jnp.bfloat16)


def tall(row):
    return jnp.broadcast_to(row, (8, LANES))


def rows_of(height):
    return lax.broadcasted_iota(jnp.int32, (height, LANES), 0).astype(jnp.float32)


def stencil_tiles(rows, height, start, columns):
    zero = jnp.zeros_like(rows)
    here = [rows == start + jnp.asarray(k, rows.dtype) for k in range(4)]
    past = [rows + jnp.asarray(height, rows.dtype) == start + jnp.asarray(k, rows.dtype) for k in range(1, 4)]
    tiles = []
    for values in columns:
        first = second = zero
        for k in range(4):
            first = jnp.where(here[k], values[k], first)
        for k in range(1, 4):
            second = jnp.where(past[k - 1], values[k], second)
        tiles.append((first, second))
    return tiles


def table_columns(block, after, tiles):
    columns = [[] for _ in tiles]
    zero = jnp.zeros_like(tiles[0][0])
    for b in range(N // 16):
        at, next_at = block == jnp.asarray(b, block.dtype), after == jnp.asarray(b, block.dtype)
        for column, (first, second) in zip(columns, tiles):
            column.append(jnp.where(at, first, jnp.where(next_at, second, zero)))
    return [jnp.concatenate(column, axis=0) for column in columns]


ANY, LOWER, UPPER, BELOW, FAR = range(5)
REACH = {ANY: (0, 4), LOWER: (0, 4), UPPER: (2, 4), BELOW: (0, 3), FAR: (0, 1)}


def plane_parts(kind, plane, parts):
    first, second, third, fourth = parts
    if kind == ANY:
        found = []
        for p in range(DEEP):
            value = 0.0
            for q in range(p + 1):
                value = jnp.where(plane == float(q), parts[p - q], value)
            found.append(value)
        return found
    low = plane < (0.5 if kind in (LOWER, FAR) else 2.5)
    if kind == LOWER:
        return [
            jnp.where(low, first, 0.0),
            jnp.where(low, second, first),
            jnp.where(low, third, second),
            jnp.where(low, fourth, third),
        ]
    if kind == UPPER:
        return [jnp.where(low, first, 0.0), jnp.where(low, second, first)]
    if kind == BELOW:
        return [
            jnp.where(low, third, second),
            jnp.where(low, fourth, third),
            jnp.where(low, 0.0, fourth),
        ]
    return [jnp.where(low, 0.0, fourth)]


def spread_rows(kind, rows, keep):
    block, after, row = places(rows[1], 16)
    keep[0], keep[1], keep[2] = block, after, row
    block, after, row = places(rows[0], 16)
    keep[3], keep[4], keep[5] = block, after, row
    for k, value in enumerate(weights_of(rows[4])):
        keep[6 + k], keep[10 + k] = row_halves(value)
    along_x = weights_of(rows[3])
    for p, depth in enumerate(plane_parts(kind, rows[2], weights_of(rows[5]))):
        for k in range(4):
            top, rest = row_halves(along_x[k] * (rows[6] * depth))
            keep[14 + 8 * p + k], keep[18 + 8 * p + k] = top, rest


def spread_planes(sources, keep, planes):
    for slot, (kind, rows) in enumerate(sources):
        spread_rows(kind, rows, keep.at[slot])
    rows16 = rows_of(16).astype(jnp.bfloat16)
    for w in range(PAIR):
        for slot, (kind, _) in enumerate(sources):
            start, stop = REACH[kind]
            count = stop - start
            left, right = [], []
            for chunk in range(HERE // LANES):
                lanes = slice(chunk * LANES, (chunk + 1) * LANES)
                row = lambda r: wide(keep[slot, r, w : w + 1, lanes])
                four = lambda r: [row(r + k) for k in range(4)]
                tiles = stencil_tiles(rows16, 16, row(2), [four(6), four(10)])
                right.append(jnp.concatenate(table_columns(row(0), row(1), tiles), axis=0))
                tiles = stencil_tiles(
                    rows16, 16, row(5), [four(14 + 4 * i) for i in range(2 * count)]
                )
                found = table_columns(row(3), row(4), tiles)
                left.append(jnp.concatenate(found[0::2] + found[1::2], axis=0))
            both = dot(jnp.concatenate(left, axis=1), jnp.concatenate(right, axis=1), (1, 1))
            height = count * N
            added = both[:height, :N] + both[:height, N:] + both[height:, :N]
            for p in range(count):
                part = added[p * N : p * N + N]
                known = planes[w][start + p]
                planes[w][start + p] = part if known is None else known + part
    return planes


def own_spread_kernel(slab_ref, own_ref, out_ref, influence_ref, keep):
    fill_influence(slab_ref, influence_ref)
    planes = [[None] * DEEP for _ in range(PAIR)]
    spread_planes([(ANY, [own_ref[r] for r in range(8)])], keep, planes)
    for w in range(PAIR):
        for p in range(DEEP):
            out_ref[w, p] = planes[w][p]


def by_core(core, first_ref, second_ref):
    pairs = [(first_ref[r], second_ref[r]) for r in range(8)]
    return (
        [jnp.where(core == 0, a, b) for a, b in pairs],
        [jnp.where(core == 0, b, a) for a, b in pairs],
    )


def spread_kernel(
    slab_ref, own_ref, near_ref, same_ref, cross_ref, y_hbm, x_hbm, out_ref, keep, y_ref, x_ref, sem
):
    copies = [
        pltpu.make_async_copy(y_hbm, y_ref, sem.at[0]),
        pltpu.make_async_copy(x_hbm, x_ref, sem.at[1]),
    ]
    for copy in copies:
        copy.start()
    core = lax.rem(slab_ref[0], 2)
    far, below = by_core(core, same_ref, cross_ref)
    planes = [[own_ref[w, p] for p in range(DEEP)] for w in range(PAIR)]
    near = [near_ref[r] for r in range(8)]
    spread_planes([(ANY, near), (BELOW, below), (FAR, far)], keep, planes)
    for copy in copies:
        copy.wait()
    stacked = jnp.concatenate(
        [jnp.concatenate([planes[0][p], planes[1][p]], axis=1) for p in range(DEEP)], axis=0
    )
    turned = times_table(stacked, y_ref)
    upright = jnp.concatenate(
        [
            jnp.concatenate([turned[b * N : b * N + N, :N], turned[b * N : b * N + N, N:]], axis=0)
            for b in range(DEEP)
        ],
        axis=1,
    )
    columns = table_times(x_ref, upright)
    for b in range(DEEP):
        out_ref[:, b] = columns[:, b * N : b * N + N].reshape(N // 4, 8, N)


def frequency(counter):
    return jnp.where(counter >= N // 2, counter - N, counter).astype(jnp.float32) / N


def fill_influence(slab_ref, out_ref):
    first = (slab_ref[0] - lax.rem(slab_ref[0], 2)) * 2
    shape = (N, N)
    freq_z = frequency(lax.broadcasted_iota(jnp.int32, shape, 0))
    freq_y = frequency(lax.broadcasted_iota(jnp.int32, shape, 1))
    flat = freq_z * freq_z + freq_y * freq_y
    for j in range(4):
        freq_x = frequency(jnp.full(shape, first + j, jnp.int32))
        squared = flat + freq_x * freq_x
        positive = squared > 0
        safe = jnp.where(positive, squared, 1.0)
        out_ref[:, j * N : j * N + N] = jnp.where(
            positive, jnp.exp(-gauss_width * squared) / (math.pi * N * N * N * safe), 0.0
        )


def column_kernel(in_ref, influence_ref, forward_ref, inverse_ref, out_ref):
    part = lambda r: in_ref[pl.ds(r, N, stride=8), :]
    columns = jnp.concatenate(
        [jnp.concatenate([part(j), part(4 + j)], axis=0) for j in range(4)], axis=1
    )
    depth = table_times(forward_ref, columns)
    influence = influence_ref[...]
    depth = jnp.concatenate([depth[:N] * influence, depth[N:] * influence], axis=0)
    back = table_times(inverse_ref, depth)
    for j in range(4):
        out_ref[pl.ds(j, N, stride=8), :] = back[:N, j * N : j * N + N]
        out_ref[pl.ds(4 + j, N, stride=8), :] = back[N:, j * N : j * N + N]


def sample_rows(kind, rows, keep):
    block, after, row = places(rows[1], 16)
    keep[0], keep[1], keep[2] = block, after, row
    for k, value in enumerate(weights_of(rows[4])):
        keep[3 + k], keep[7 + k] = row_halves(value)
    for k, value in enumerate(slopes_of(rows[4])):
        keep[11 + k], keep[15 + k] = row_halves(value)
    block, after, row = places(rows[0], 8)
    keep[19], keep[20], keep[21] = block, after, row
    for k, (value, slope) in enumerate(zip(weights_of(rows[3]), slopes_of(rows[3]))):
        keep[22 + k], keep[26 + k] = value, slope
    for p, depth in enumerate(plane_parts(kind, rows[2], weights_of(rows[5]))):
        keep[30 + p] = depth
    for p, steep in enumerate(plane_parts(kind, rows[2], slopes_of(rows[5]))):
        keep[34 + p] = steep
    keep[38], keep[39] = rows[6], rows[7]


def sample_kernel(
    slab_ref,
    in_ref,
    own_ref,
    near_ref,
    same_ref,
    cross_ref,
    x_ref,
    y_ref,
    own_out,
    near_out,
    same_out,
    cross_out,
    sum_out,
    keep,
    forces,
    sums,
):
    core = lax.rem(slab_ref[0], 2)
    columns = jnp.concatenate([in_ref[:, b].reshape(2 * N, N) for b in range(DEEP)], axis=1)
    upright = table_times(x_ref, columns)
    flat = jnp.concatenate(
        [
            jnp.concatenate([upright[:N, b * N : b * N + N], upright[N:, b * N : b * N + N]], axis=1)
            for b in range(DEEP)
        ],
        axis=0,
    )
    pairs = times_table(flat, y_ref)
    lower, upper = by_core(core, own_ref, near_ref)
    far, below = by_core(core, same_ref, cross_ref)
    sources = ((LOWER, lower), (UPPER, upper), (BELOW, below), (FAR, far))
    for slot, (kind, rows) in enumerate(sources):
        sample_rows(kind, rows, keep.at[slot])
    rows16 = rows_of(16).astype(jnp.bfloat16)
    rows8 = rows_of(8)
    for w in range(PAIR):
        planes = jnp.concatenate(halves(pairs[:, w * N : w * N + N]), axis=1)
        energy = jnp.zeros((1, LANES), jnp.float32)
        slope = jnp.zeros((1, LANES), jnp.float32)
        for slot, (kind, _) in enumerate(sources):
            start, stop = REACH[kind]
            count = stop - start
            tops, rests = [], []
            for chunk in range(HERE // LANES):
                lanes = slice(chunk * LANES, (chunk + 1) * LANES)
                row = lambda r: wide(keep[slot, r, w : w + 1, lanes])
                four = lambda r: [row(r + k) for k in range(4)]
                tiles = stencil_tiles(rows16, 16, row(2), [four(3 + 4 * i) for i in range(4)])
                found = table_columns(row(0), row(1), tiles)
                tops.append(jnp.concatenate([found[0], found[2]], axis=1))
                rests.append(jnp.concatenate([found[1], found[3]], axis=1))
            tops = jnp.concatenate(tops, axis=1)
            rests = jnp.concatenate(rests, axis=1)
            used = planes[start * N : stop * N]
            levels = dot(used, jnp.concatenate([tops, tops], axis=0)) + dot(used[:, :N], rests)
            for chunk in range(HERE // LANES):
                lanes = slice(chunk * LANES, (chunk + 1) * LANES)
                row = lambda r: tall(keep[slot, r, w : w + 1, lanes])
                four = lambda r: [row(r + k) for k in range(4)]
                block, after = row(19), row(20)
                tiles = stencil_tiles(rows8, 8, row(21), [four(22), four(26)])
                near = [[None] * 2 for _ in range(2 * count)]
                for b in range(N // 8):
                    at, next_at = block == float(b), after == float(b)
                    for q in range(2 * count):
                        p, slant = q // 2, q % 2
                        level = levels[
                            p * N + b * 8 : p * N + b * 8 + 8,
                            (2 * chunk + slant) * LANES : (2 * chunk + slant + 1) * LANES,
                        ]
                        if b == 0:
                            near[q] = [level, level]
                        else:
                            near[q][0] = jnp.where(at, level, near[q][0])
                            near[q][1] = jnp.where(next_at, level, near[q][1])
                total = [jnp.zeros((8, LANES), jnp.float32) for _ in range(4)]
                for half in range(2):
                    along, along_dx = tiles[0][half], tiles[1][half]
                    plain = near[0][half] * row(30)
                    over_z = near[0][half] * row(34)
                    over_y = near[1][half] * row(30)
                    for p in range(1, count):
                        plain = plain + near[2 * p][half] * row(30 + p)
                        over_z = over_z + near[2 * p][half] * row(34 + p)
                        over_y = over_y + near[2 * p + 1][half] * row(30 + p)
                    total[0] = total[0] + along * plain
                    total[1] = total[1] + along_dx * plain
                    total[2] = total[2] + along * over_y
                    total[3] = total[3] + along * over_z
                total = [jnp.sum(t, axis=0, keepdims=True) for t in total]
                charge = keep[slot, 38, w : w + 1, lanes]
                for d in range(3):
                    forces[slot, d, w : w + 1, lanes] = -charge * total[1 + d]
                energy = energy + charge * total[0]
                slope = slope + keep[slot, 39, w : w + 1, lanes] * total[0]
        sums[w : w + 1, :] = energy
        sums[PAIR + w : PAIR + w + 1, :] = slope
    own_out[...] = jnp.where(core == 0, forces[0], forces[1])
    near_out[...] = jnp.where(core == 0, forces[1], forces[0])
    same_out[...] = jnp.where(core == 0, forces[3], forces[2])
    cross_out[...] = jnp.where(core == 0, forces[2], forces[3])
    added = jnp.sum(sums[...], axis=1, keepdims=True)
    shape = (2 * PAIR, LANES)
    row = lax.broadcasted_iota(jnp.int32, shape, 0)
    place = PAIR * core + jnp.where(row < PAIR, row, row - PAIR + WINDOWS)
    here = lax.broadcasted_iota(jnp.int32, shape, 1) == place
    line = jnp.sum(jnp.where(here, added, 0.0), axis=0, keepdims=True)
    sum_out[...] = jnp.broadcast_to(line, (SLABS, LANES))


def finish_kernel(
    slab_ref, own_ref, near_ref, same_ref, cross_ref, sum_ref, force_out, energy_out, slope_out
):
    core = lax.rem(slab_ref[0], 2)
    mine = own_ref[...] + same_ref[...]
    other = near_ref[...] + cross_ref[...]
    force_out[:, :PAIR] = jnp.where(core == 0, mine, other)
    force_out[:, PAIR:] = jnp.where(core == 0, other, mine)
    line = jnp.sum(sum_ref[...], axis=0, keepdims=True)
    lane = lax.broadcasted_iota(jnp.int32, (1, LANES), 1)
    for w in range(WINDOWS):
        energy_out[w] = jnp.sum(jnp.where(lane == w, line, 0.0)) * (0.5 / ATOMS)
        slope_out[w] = jnp.sum(jnp.where(lane == WINDOWS + w, line, 0.0)) * (1.0 / ATOMS)


in_vmem = pl.BlockSpec(memory_space=pltpu.VMEM)
in_smem = pl.BlockSpec(memory_space=pltpu.SMEM)
in_hbm = pl.BlockSpec(memory_space=pltpu.HBM)
table_scratch = pltpu.VMEM((2, 2 * N, 2 * N), jnp.bfloat16)


def far_away(array):
    return pltpu.with_memory_space_constraint(array, pltpu.HBM)


def f32(*shape):
    return jax.ShapeDtypeStruct(shape, jnp.float32)


def run(kernel, out_shape, in_specs, operands, scratch=(), mib=16):
    several = isinstance(out_shape, tuple)
    return pl.pallas_call(
        kernel,
        out_shape=out_shape,
        in_specs=in_specs,
        out_specs=(in_vmem,) * len(out_shape) if several else in_vmem,
        scratch_shapes=list(scratch),
        compiler_params=pltpu.CompilerParams(vmem_limit_bytes=mib << 20),
        name=kernel.__name__,
    )(*operands)


def moved(value, pairs, back=False):
    return lax.ppermute(value, "slab", [pair[::-1] if back else pair for pair in pairs])


TO_PARTNER = [(d, d ^ 1) for d in range(SLABS)]
UP_SAME = [(d, (d + 2) % SLABS) for d in range(SLABS)]
UP_CROSS = [(d, ((d ^ 1) + 2) % SLABS) for d in range(SLABS)]
CORES = [list(range(c, SLABS, 2)) for c in range(2)]


def exchanged(value):
    return lax.all_to_all(value, "slab", 0, 0, tiled=True, axis_index_groups=CORES)


def body(lambdas, charge_a, charge_b, perturbed, grid_index, spline_weights, spline_slopes):
    slab = lax.axis_index("slab").reshape(1)
    inputs = tuple(
        far_away(a)
        for a in (lambdas, charge_a, charge_b, perturbed, grid_index, spline_weights)
    )
    atoms = f32(8, PAIR, HERE)
    own, other = run(
        pack_kernel,
        (atoms, atoms),
        [in_smem] + [in_hbm] * 6,
        (slab, *inputs),
        [pltpu.SMEM((WINDOWS,), jnp.float32)]
        + [pltpu.VMEM(a.shape, a.dtype) for a in inputs[1:]]
        + [pltpu.SemaphoreType.DMA((6,))],
        mib=4,
    )
    near = moved(other, TO_PARTNER)
    same = moved(own, UP_SAME)
    cross = moved(other, UP_CROSS)
    kept = lambda count, rows: pltpu.VMEM((count, rows, PAIR, HERE), jnp.float32)
    from_own, influence = run(
        own_spread_kernel,
        (f32(PAIR, DEEP, N, N), f32(N, 4 * N)),
        [in_smem, in_vmem],
        (slab, own),
        [kept(1, 46)],
    )
    spectrum = run(
        spread_kernel,
        f32(CHIPS, DEEP, 8, N),
        [in_smem] + [in_vmem] * 4 + [in_hbm] * 2,
        (
            slab,
            from_own,
            near,
            same,
            cross,
            far_away(jnp.asarray(Y_FORWARD)),
            far_away(jnp.asarray(X_FORWARD)),
        ),
        [kept(3, 46), table_scratch, table_scratch, pltpu.SemaphoreType.DMA((2,))],
    )
    columns = exchanged(spectrum.reshape(CHIPS, 8 * DEEP, N))
    columns = run(
        column_kernel,
        f32(8 * N, N),
        [in_vmem] * 4,
        (columns.reshape(8 * N, N), influence, Z_FORWARD, Z_INVERSE),
        mib=8,
    )
    levels = exchanged(columns.reshape(CHIPS, 8 * DEEP, N))
    part = f32(3, PAIR, HERE)
    mine, for_near, for_same, for_cross, sums = run(
        sample_kernel,
        (part, part, part, part, f32(SLABS, N)),
        [in_smem] + [in_vmem] * 7,
        (slab, levels.reshape(CHIPS, DEEP, 8, N), own, near, same, cross, X_INVERSE, Y_INVERSE),
        [
            kept(4, 40),
            pltpu.VMEM((4, 3, PAIR, HERE), jnp.float32),
            pltpu.VMEM((2 * PAIR, LANES), jnp.float32),
        ],
    )
    from_near = moved(for_near, TO_PARTNER, back=True)
    from_same = moved(for_same, UP_SAME, back=True)
    from_cross = moved(for_cross, UP_CROSS, back=True)
    sums = lax.all_to_all(sums.reshape(SLABS, 1, N), "slab", 0, 0, tiled=True)
    return pl.pallas_call(
        finish_kernel,
        out_shape=(f32(3, WINDOWS, HERE), f32(WINDOWS), f32(WINDOWS)),
        in_specs=[in_smem] + [in_vmem] * 5,
        out_specs=(in_vmem, in_smem, in_smem),
        compiler_params=pltpu.CompilerParams(vmem_limit_bytes=4 << 20),
        name="finish_kernel",
    )(slab, mine, from_near, from_same, from_cross, sums.reshape(SLABS, N))


def solution(mesh):
    return jax.shard_map(
        body,
        mesh=mesh,
        in_specs=(
            P("win"),
            P("win", "slab"),
            P("win", "slab"),
            P("win", "slab"),
            P(None, "win", "slab"),
            P(None, None, "win", "slab"),
            P(None, None, "win", "slab"),
        ),
        out_specs=(P(None, "win", "slab"), P("win"), P("win")),
        check_vma=False,
    )
```

time: 71.6 us -> 67.2 us (0.939); the launches traced: 70.5 us -> 66.9 us
  blocking collectives: 36.5 us -> 27 us
  waiting for transfers between devices: 4.27 us -> 8.22 us
  starting transfers between devices: 15 us -> 18.8 us
  local copies, waits for them, and re-layouts: 1.85 us -> 0.02 us
    all_to_all x2, blocking collectives: 36.5 us -> 27 us  [exchanged(): lax.all_to_all(value, 'slab', 0, 0, tiled=True, axis_index_groups=CORES)]
    ppermute x4 -> x6, waiting for transfers between devices: 3.81 us -> 8.22 us  [moved(): lax.ppermute(value, 'slab', [pair[::-1] if back else pair for pair in pai...]
    all_to_all x1, starting transfers between devices: 4.44 us -> 7.92 us  [body(): sums = lax.all_to_all(sums.reshape(SLABS, 1, N), 'slab', 0, 0, tiled=True)]
    unnamed x12 -> x6, local copies, waits for them, and re-layouts: 1.85 us -> 0.02 us
    ppermute x4 -> x6, starting transfers between devices: 10.6 us -> 10.9 us  [moved(): lax.ppermute(value, 'slab', [pair[::-1] if back else pair for pair in pai...]
  transfers between devices with their start and end apart: 5 -> 7, of which waited for: 3 -> 4; matrix products, arithmetic and copies ran while one was open for 0% -> 0% of each run, Pallas kernels for 2% -> 1%
where the time goes in v3:
time: 67.2 us; the launch traced here: 66.9 us
  blocking collectives  27 us (40%)
  starting transfers between devices  18.8 us (28%)
  Pallas kernels  12.2 us (18%)
  waiting for transfers between devices  8.22 us (12%)
  between operations  0.71 us (1%)
    all_to_all x2, blocking collectives, exchanged(): lax.all_to_all(value, 'slab', 0, 0, tiled=True, axis_index_groups=CORES)  27 us
    pallas_call x5, Pallas kernels, run(): pl.pallas_call(kernel, out_shape=out_shape, in_specs=in_specs, out_specs=...  11.5 us
    ppermute x6, starting transfers between devices, moved(): lax.ppermute(value, 'slab', [pair[::-1] if back else pair for pair in pai...  10.9 us
    ppermute x6, waiting for transfers between devices, moved(): lax.ppermute(value, 'slab', [pair[::-1] if back else pair for pair in pai...  8.22 us
    all_to_all x1, starting transfers between devices, body(): sums = lax.all_to_all(sums.reshape(SLABS, 1, N), 'slab', 0, 0, tiled=True)  7.92 us
  transfers between devices with their start and end apart: 7, of which 4 were waited for; matrix products, arithmetic and copies ran while one was open for 0% of the time, Pallas kernels for 1%

profile of v3, /device:TPU:1, one launch (start us, length us, event | category | flops | bytes accessed | tf_op | source)
XLA Modules:
  0.0 66.9 jit_solution(9791037783178341396)
XLA Ops:
  0.6 1.0 %pack_kernel.1 = (f32[8,2,512]{2,1,0:T(2,128)S(1)}, f32[8,2,512]{2,1,0:T(2,128)S(1)}) custom-call(s32[1]{0:T(128)} %bitcast.slab_ref, f32[4]{0:T(128)} %refs_0_.1, f32[4,512]{1,0:T(4,128)} %refs_1_.1, f32[4,512]{1,0:T(4,128)} %refs_2_.1, s32[4,512]{1,0:T(4,128)} %refs_3_.1, s32[3,4,512]{2,1,0:T(4,128)} %refs_4_.1, f32[3,4,4,512]{3,2,1,0:T(4,128)} %refs_5_.1), custom_call_target="tpu_custom_call" | custom-call | tf_op jit(solution)/shard_map/pack_kernel/pallas_call | solution.py:491
  1.7 3.1 %collective-permute-start.2 = (f32[8,2,512]{2,1,0:T(2,128)S(1)}, f32[8,2,512]{2,1,0:T(2,128)S(1)}, u32[]{:S(2)}, u32[]{:S(2)}) collective-permute-start(f32[8,2,512]{2,1,0:T(2,128)S(1)} %get-tuple-element.14), channel_id=1, source_target_pairs={{0,3},{1,2},{2,5},{3,4},{4,7},{5,6},{6,9},{7,8},{8,11},{9,10},{10,... | collective-permute-start | bytes 98312 | tf_op jit(solution)/shard_map/ppermute | solution.py:503
  4.8 0.3 collective-permute-start
  5.1 0.5 collective-permute-start.1
  5.5 1.0 %own_spread_kernel.1 = (f32[2,4,128,128]{3,2,1,0:T(8,128)S(1)}, f32[128,512]{1,0:T(8,128)S(1)}) custom-call(s32[1]{0:T(128)} %bitcast.slab_ref, f32[8,2,512]{2,1,0:T(2,128)S(1)} %get-tuple-element.12.own_ref), custom_call_target="tpu_custom_call" | custom-call | tf_op jit(solution)/shard_map/own_spread_kernel/pallas_call | solution.py:491
  6.5 4.5 %collective-permute-done.2.cross_ref = f32[8,2,512]{2,1,0:T(2,128)S(1)} collective-permute-done((f32[8,2,512]{2,1,0:T(2,128)S(1)}, f32[8,2,512]{2,1,0:T(2,128)S(1)}, u32[]{:S(2)}, u32[]{:S(2)}) %collective-permute-start.2) | collective-permute-done | bytes 32800 | tf_op jit(solution)/shard_map/ppermute | solution.py:503
  11.0 0.0 collective-permute-done.near_ref
  11.0 1.2 %collective-permute-done.1.same_ref = f32[8,2,512]{2,1,0:T(2,128)S(1)} collective-permute-done((f32[8,2,512]{2,1,0:T(2,128)S(1)}, f32[8,2,512]{2,1,0:T(2,128)S(1)}, u32[]{:S(2)}, u32[]{:S(2)}) %collective-permute-start.1) | collective-permute-done | bytes 32800 | tf_op jit(solution)/shard_map/ppermute | solution.py:503
  12.2 3.8 %spread_kernel.1 = f32[32,4,8,128]{3,2,1,0:T(8,128)S(1)} custom-call(s32[1]{0:T(128)} %bitcast.slab_ref, f32[2,4,128,128]{3,2,1,0:T(8,128)S(1)} %get-tuple-element.13.own_ref, f32[8,2,512]{2,1,0:T(2,128)S(1)} %collective-permute-done.near_ref, f32[8,2,512]{2,1,0:T(2,128)S(1)} %collective-permute-done.1.same_ref, ...), custom_call_target="tpu_custom_call" | custom-call | tf_op jit(solution)/shard_map/spread_kernel/pallas_call | solution.py:491
  16.0 0.0 copy-start
  16.0 0.0 copy-start.1
  16.0 13.8 %all_to_all.15 = f32[32,32,128]{2,1,0:T(8,128)S(1)} all-to-all(f32[32,32,128]{2,1,0:T(8,128)S(1)} %bitcast.12), channel_id=1, replica_groups={{0,2,4,6,8,10,12,14,16,18,20,22,24,26,28,30,32,34,36,38,40,42,44,46,48,..., dimensions={0} | all-to-all | bytes 1048576 | tf_op jit(solution)/shard_map/all_to_all | solution.py:513
  29.8 0.0 copy-done
  29.8 0.0 copy-done.1
  29.8 0.8 %column_kernel.1 = f32[1024,128]{1,0:T(8,128)S(1)} custom-call(f32[1024,128]{1,0:T(8,128)S(1)} %bitcast.9, f32[128,512]{1,0:T(8,128)S(1)} %get-tuple-element.15.influence_ref, bf16[2,256,256]{2,1,0:T(8,128)(2,1)S(1)} %copy-done, bf16[2,256,256]{2,1,0:T(8,128)(2,1)S(1)} %copy-done.1), custom_call_target="tpu_custom_call" | custom-call | tf_op jit(solution)/shard_map/column_kernel/pallas_call | solution.py:491
  30.7 0.0 copy-start.2
  30.7 13.2 %all_to_all.16 = f32[32,32,128]{2,1,0:T(8,128)S(1)} all-to-all(f32[32,32,128]{2,1,0:T(8,128)S(1)} %bitcast.10), channel_id=1, replica_groups={{0,2,4,6,8,10,12,14,16,18,20,22,24,26,28,30,32,34,36,38,40,42,44,46,48,..., dimensions={0} | all-to-all | bytes 1048576 | tf_op jit(solution)/shard_map/all_to_all | solution.py:513
  43.8 0.0 copy-done.2
  43.8 4.9 %sample_kernel.1 = (f32[3,2,512]{2,1,0:T(2,128)S(1)}, f32[3,2,512]{2,1,0:T(2,128)S(1)}, f32[3,2,512]{2,1,0:T(2,128)S(1)}, f32[3,2,512]{2,1,0:T(2,128)S(1)}, f32[64,128]{1,0:T(8,128)}) custom-call(s32[1]{0:T(128)} %bitcast.slab_ref, f32[32,4,8,128]{3,2,1,0:T(8,128)S(1)} %bitcast.11, f32[8,2,512]{2,1,0:T(2,128)S(1)} %get-tuple-element.12.own_ref, ...), custom_call_target="tpu_custom_call" | custom-call | tf_op jit(solution)/shard_map/sample_kernel/pallas_call | solution.py:491
  48.7 7.9 %all-to-all-start.2 = ((f32[64,1,128]{2,1,0:T(1,128)}), f32[64,1,128]{2,1,0:T(1,128)S(1)}, u32[]{:S(2)}, u32[]{:S(2)}) async-start(f32[64,1,128]{2,1,0:T(1,128)} %bitcast.6), calls=%async_computation.2 | async-start | bytes 65536 | tf_op jit(solution)/shard_map/all_to_all | solution.py:583
  56.6 0.7 collective-permute-start.3
  57.3 5.8 %collective-permute-start.4 = (f32[3,2,512]{2,1,0:T(2,128)S(1)}, f32[3,2,512]{2,1,0:T(2,128)S(1)}, u32[]{:S(2)}, u32[]{:S(2)}) collective-permute-start(f32[3,2,512]{2,1,0:T(2,128)S(1)} %get-tuple-element.18), channel_id=1, source_target_pairs={{2,0},{3,1},{4,2},{5,3},{6,4},{7,5},{8,6},{9,7},{10,8},{11,9},{12,... | collective-permute-start | bytes 36872 | tf_op jit(solution)/shard_map/ppermute | solution.py:503
  63.1 0.6 collective-permute-start.5
  63.7 0.0 collective-permute-done.3.near_ref
  63.7 0.3 collective-permute-done.4.same_ref
  63.9 2.3 %collective-permute-done.5.cross_ref = f32[3,2,512]{2,1,0:T(2,128)S(1)} collective-permute-done((f32[3,2,512]{2,1,0:T(2,128)S(1)}, f32[3,2,512]{2,1,0:T(2,128)S(1)}, u32[]{:S(2)}, u32[]{:S(2)}) %collective-permute-start.5) | collective-permute-done | bytes 12320 | tf_op jit(solution)/shard_map/ppermute | solution.py:503
  66.2 0.0 all-to-all-done.2
  66.2 0.7 finish_kernel.1
Async XLA Ops:
  1.7 9.3 %collective-permute-start.2 = (f32[8,2,512]{2,1,0:T(2,128)S(1)}, f32[8,2,512]{2,1,0:T(2,128)S(1)}, u32[]{:S(2)}, u32[]{:S(2)}) collective-permute-start(f32[8,2,512]{2,1,0:T(2,128)S(1)} %get-tuple-element.14), channel_id=1, source_target_pairs={{0,3},{1,2},{2,5},{3,4},{4,7},{5,6},{6,9},{7,8},{8,11},{9,10},{10,... | collective-permute-start | bytes 98312 | tf_op jit(solution)/shard_map/ppermute | solution.py:503
  4.8 6.2 %collective-permute-start = (f32[8,2,512]{2,1,0:T(2,128)S(1)}, f32[8,2,512]{2,1,0:T(2,128)S(1)}, u32[]{:S(2)}, u32[]{:S(2)}) collective-permute-start(f32[8,2,512]{2,1,0:T(2,128)S(1)} %get-tuple-element.14), channel_id=1, source_target_pairs={{0,1},{1,0},{2,3},{3,2},{4,5},{5,4},{6,7},{7,6},{8,9},{9,8},{10,11... | collective-permute-start | bytes 98312 | tf_op jit(solution)/shard_map/ppermute | solution.py:503
  5.1 7.1 %collective-permute-start.1 = (f32[8,2,512]{2,1,0:T(2,128)S(1)}, f32[8,2,512]{2,1,0:T(2,128)S(1)}, u32[]{:S(2)}, u32[]{:S(2)}) collective-permute-start(f32[8,2,512]{2,1,0:T(2,128)S(1)} %get-tuple-element.12.own_ref), channel_id=1, source_target_pairs={{0,2},{1,3},{2,4},{3,5},{4,6},{5,7},{6,8},{7,9},{8,10},{9,11},{10,... | collective-permute-start | bytes 98312 | tf_op jit(solution)/shard_map/ppermute | solution.py:503
  16.0 13.8 %copy-start = (bf16[2,256,256]{2,1,0:T(8,128)(2,1)S(1)}, bf16[2,256,256]{2,1,0:T(8,128)(2,1)}, u32[]{:S(2)}) copy-start(bf16[2,256,256]{2,1,0:T(8,128)(2,1)} %constant.14.clone.forward_ref.y_ref) | copy-start | bytes 786436
  16.0 13.8 %copy-start.1 = (bf16[2,256,256]{2,1,0:T(8,128)(2,1)S(1)}, bf16[2,256,256]{2,1,0:T(8,128)(2,1)}, u32[]{:S(2)}) copy-start(bf16[2,256,256]{2,1,0:T(8,128)(2,1)} %constant.12.clone.y_hbm.inverse_ref) | copy-start | bytes 786436
  30.7 13.2 %copy-start.2 = (bf16[2,256,256]{2,1,0:T(8,128)(2,1)S(1)}, bf16[2,256,256]{2,1,0:T(8,128)(2,1)}, u32[]{:S(2)}) copy-start(bf16[2,256,256]{2,1,0:T(8,128)(2,1)} %constant.15.clone.x_ref) | copy-start | bytes 786436
  48.7 17.5 %all-to-all-start.2 = ((f32[64,1,128]{2,1,0:T(1,128)}), f32[64,1,128]{2,1,0:T(1,128)S(1)}, u32[]{:S(2)}, u32[]{:S(2)}) async-start(f32[64,1,128]{2,1,0:T(1,128)} %bitcast.6), calls=%async_computation.2 | async-start | bytes 65536 | tf_op jit(solution)/shard_map/all_to_all | solution.py:583
  56.6 7.0 %collective-permute-start.3 = (f32[3,2,512]{2,1,0:T(2,128)S(1)}, f32[3,2,512]{2,1,0:T(2,128)S(1)}, u32[]{:S(2)}, u32[]{:S(2)}) collective-permute-start(f32[3,2,512]{2,1,0:T(2,128)S(1)} %get-tuple-element.17), channel_id=1, source_target_pairs={{1,0},{0,1},{3,2},{2,3},{5,4},{4,5},{7,6},{6,7},{9,8},{8,9},{11,10... | collective-permute-start | bytes 36872 | tf_op jit(solution)/shard_map/ppermute | solution.py:503
  57.3 6.6 %collective-permute-start.4 = (f32[3,2,512]{2,1,0:T(2,128)S(1)}, f32[3,2,512]{2,1,0:T(2,128)S(1)}, u32[]{:S(2)}, u32[]{:S(2)}) collective-permute-start(f32[3,2,512]{2,1,0:T(2,128)S(1)} %get-tuple-element.18), channel_id=1, source_target_pairs={{2,0},{3,1},{4,2},{5,3},{6,4},{7,5},{8,6},{9,7},{10,8},{11,9},{12,... | collective-permute-start | bytes 36872 | tf_op jit(solution)/shard_map/ppermute | solution.py:503
  63.1 3.1 %collective-permute-start.5 = (f32[3,2,512]{2,1,0:T(2,128)S(1)}, f32[3,2,512]{2,1,0:T(2,128)S(1)}, u32[]{:S(2)}, u32[]{:S(2)}) collective-permute-start(f32[3,2,512]{2,1,0:T(2,128)S(1)} %get-tuple-element.19), channel_id=1, source_target_pairs={{3,0},{2,1},{5,2},{4,3},{7,4},{6,5},{9,6},{8,7},{11,8},{10,9},{13,... | collective-permute-start | bytes 36872 | tf_op jit(solution)/shard_map/ppermute | solution.py:503

commit v4 on v3

--- a/solution.py
+++ b/solution.py
@@ -87,7 +87,8 @@
     return (-0.5 * v * v, (1.5 * u - 2.0) * u, (2.0 - 1.5 * v) * v, 0.5 * u * u)
 
 
-def pack_kernel(slab_ref, *refs):
+def pack_kernel(*refs):
+    slab = lax.axis_index("slab")
     sources, (mine_ref, other_ref), landed, sem = refs[:6], refs[6:8], refs[8:14], refs[14]
     copies = [
         pltpu.make_async_copy(source, target, sem.at[i])
@@ -100,8 +101,8 @@
     lambda_ref, a_ref, b_ref, flag_ref, index_ref, weight_ref = landed
     flags = flag_ref[...].astype(jnp.float32)
     steps = flags * (b_ref[...] - a_ref[...])
-    core = lax.rem(slab_ref[0], 2)
-    first = (slab_ref[0] - core) * 2
+    core = lax.rem(slab, 2)
+    first = (slab - core) * 2
     row = lax.broadcasted_iota(jnp.int32, (WINDOWS, HERE), 0)
     scale = jnp.zeros((WINDOWS, HERE), jnp.float32)
     for w in range(WINDOWS):
@@ -245,10 +246,11 @@
     return planes
 
 
-def own_spread_kernel(slab_ref, own_ref, out_ref, influence_ref, keep):
-    fill_influence(slab_ref, influence_ref)
+def chip_spread_kernel(own_ref, near_ref, out_ref, influence_ref, keep):
+    fill_influence(influence_ref)
     planes = [[None] * DEEP for _ in range(PAIR)]
-    spread_planes([(ANY, [own_ref[r] for r in range(8)])], keep, planes)
+    here = [(ANY, [ref[r] for r in range(8)]) for ref in (own_ref, near_ref)]
+    spread_planes(here, keep, planes)
     for w in range(PAIR):
         for p in range(DEEP):
             out_ref[w, p] = planes[w][p]
@@ -263,7 +265,7 @@
 
 
 def spread_kernel(
-    slab_ref, own_ref, near_ref, same_ref, cross_ref, y_hbm, x_hbm, out_ref, keep, y_ref, x_ref, sem
+    chip_ref, same_ref, cross_ref, y_hbm, x_hbm, out_ref, keep, y_ref, x_ref, sem
 ):
     copies = [
         pltpu.make_async_copy(y_hbm, y_ref, sem.at[0]),
@@ -271,11 +273,10 @@
     ]
     for copy in copies:
         copy.start()
-    core = lax.rem(slab_ref[0], 2)
+    core = lax.rem(lax.axis_index("slab"), 2)
     far, below = by_core(core, same_ref, cross_ref)
-    planes = [[own_ref[w, p] for p in range(DEEP)] for w in range(PAIR)]
-    near = [near_ref[r] for r in range(8)]
-    spread_planes([(ANY, near), (BELOW, below), (FAR, far)], keep, planes)
+    planes = [[chip_ref[w, p] for p in range(DEEP)] for w in range(PAIR)]
+    spread_planes([(BELOW, below), (FAR, far)], keep, planes)
     for copy in copies:
         copy.wait()
     stacked = jnp.concatenate(
@@ -298,8 +299,9 @@
     return jnp.where(counter >= N // 2, counter - N, counter).astype(jnp.float32) / N
 
 
-def fill_influence(slab_ref, out_ref):
-    first = (slab_ref[0] - lax.rem(slab_ref[0], 2)) * 2
+def fill_influence(out_ref):
+    slab = lax.axis_index("slab")
+    first = (slab - lax.rem(slab, 2)) * 2
     shape = (N, N)
     freq_z = frequency(lax.broadcasted_iota(jnp.int32, shape, 0))
     freq_y = frequency(lax.broadcasted_iota(jnp.int32, shape, 1))
@@ -347,7 +349,6 @@
 
 
 def sample_kernel(
-    slab_ref,
     in_ref,
     own_ref,
     near_ref,
@@ -364,7 +365,7 @@
     forces,
     sums,
 ):
-    core = lax.rem(slab_ref[0], 2)
+    core = lax.rem(lax.axis_index("slab"), 2)
     columns = jnp.concatenate([in_ref[:, b].reshape(2 * N, N) for b in range(DEEP)], axis=1)
     upright = table_times(x_ref, columns)
     flat = jnp.concatenate(
@@ -458,9 +459,9 @@
 
 
 def finish_kernel(
-    slab_ref, own_ref, near_ref, same_ref, cross_ref, sum_ref, force_out, energy_out, slope_out
+    own_ref, near_ref, same_ref, cross_ref, sum_ref, force_out, energy_out, slope_out
 ):
-    core = lax.rem(slab_ref[0], 2)
+    core = lax.rem(lax.axis_index("slab"), 2)
     mine = own_ref[...] + same_ref[...]
     other = near_ref[...] + cross_ref[...]
     force_out[:, :PAIR] = jnp.where(core == 0, mine, other)
@@ -514,7 +515,6 @@
 
 
 def body(lambdas, charge_a, charge_b, perturbed, grid_index, spline_weights, spline_slopes):
-    slab = lax.axis_index("slab").reshape(1)
     inputs = tuple(
         far_away(a)
         for a in (lambdas, charge_a, charge_b, perturbed, grid_index, spline_weights)
@@ -523,8 +523,8 @@
     own, other = run(
         pack_kernel,
         (atoms, atoms),
-        [in_smem] + [in_hbm] * 6,
-        (slab, *inputs),
+        [in_hbm] * 6,
+        inputs,
         [pltpu.SMEM((WINDOWS,), jnp.float32)]
         + [pltpu.VMEM(a.shape, a.dtype) for a in inputs[1:]]
         + [pltpu.SemaphoreType.DMA((6,))],
@@ -534,27 +534,25 @@
     same = moved(own, UP_SAME)
     cross = moved(other, UP_CROSS)
     kept = lambda count, rows: pltpu.VMEM((count, rows, PAIR, HERE), jnp.float32)
-    from_own, influence = run(
-        own_spread_kernel,
+    from_chip, influence = run(
+        chip_spread_kernel,
         (f32(PAIR, DEEP, N, N), f32(N, 4 * N)),
-        [in_smem, in_vmem],
-        (slab, own),
-        [kept(1, 46)],
+        [in_vmem] * 2,
+        (own, near),
+        [kept(2, 46)],
     )
     spectrum = run(
         spread_kernel,
         f32(CHIPS, DEEP, 8, N),
-        [in_smem] + [in_vmem] * 4 + [in_hbm] * 2,
+        [in_vmem] * 3 + [in_hbm] * 2,
         (
-            slab,
-            from_own,
-            near,
+            from_chip,
             same,
             cross,
             far_away(jnp.asarray(Y_FORWARD)),
             far_away(jnp.asarray(X_FORWARD)),
         ),
-        [kept(3, 46), table_scratch, table_scratch, pltpu.SemaphoreType.DMA((2,))],
+        [kept(2, 46), table_scratch, table_scratch, pltpu.SemaphoreType.DMA((2,))],
     )
     columns = exchanged(spectrum.reshape(CHIPS, 8 * DEEP, N))
     columns = run(
@@ -569,8 +567,8 @@
     mine, for_near, for_same, for_cross, sums = run(
         sample_kernel,
         (part, part, part, part, f32(SLABS, N)),
-        [in_smem] + [in_vmem] * 7,
-        (slab, levels.reshape(CHIPS, DEEP, 8, N), own, near, same, cross, X_INVERSE, Y_INVERSE),
+        [in_vmem] * 7,
+        (levels.reshape(CHIPS, DEEP, 8, N), own, near, same, cross, X_INVERSE, Y_INVERSE),
         [
             kept(4, 40),
             pltpu.VMEM((4, 3, PAIR, HERE), jnp.float32),
@@ -584,11 +582,11 @@
     return pl.pallas_call(
         finish_kernel,
         out_shape=(f32(3, WINDOWS, HERE), f32(WINDOWS), f32(WINDOWS)),
-        in_specs=[in_smem] + [in_vmem] * 5,
+        in_specs=[in_vmem] * 5,
         out_specs=(in_vmem, in_smem, in_smem),
         compiler_params=pltpu.CompilerParams(vmem_limit_bytes=4 << 20),
         name="finish_kernel",
-    )(slab, mine, from_near, from_same, from_cross, sums.reshape(SLABS, N))
+    )(mine, from_near, from_same, from_cross, sums.reshape(SLABS, N))
 
 
 def solution(mesh):

time: 67.2 us -> 65.8 us (0.979)
  Pallas kernels: 12.2 us -> 11.2 us
    pallas_call x5, Pallas kernels: 11.5 us -> 10.6 us  [run(): pl.pallas_call(kernel, out_shape=out_shape, in_specs=in_specs, out_specs=...]
  transfers between devices with their start and end apart: 7 -> 7, of which waited for: 4 -> 4; matrix products, arithmetic and copies ran while one was open for 0% -> 0% of each run, Pallas kernels for 1% -> 3%
where the time goes in v4:
time: 65.8 us; the launch traced here: 65.5 us
  blocking collectives  27.3 us (41%)
  starting transfers between devices  18.4 us (28%)
  Pallas kernels  11.2 us (17%)
  waiting for transfers between devices  7.86 us (12%)
  between operations  0.7 us (1%)
    all_to_all x2, blocking collectives, exchanged(): lax.all_to_all(value, 'slab', 0, 0, tiled=True, axis_index_groups=CORES)  27.3 us
    ppermute x6, starting transfers between devices, moved(): lax.ppermute(value, 'slab', [pair[::-1] if back else pair for pair in pai...  11 us
    pallas_call x5, Pallas kernels, run(): pl.pallas_call(kernel, out_shape=out_shape, in_specs=in_specs, out_specs=...  10.6 us
    ppermute x6, waiting for transfers between devices, moved(): lax.ppermute(value, 'slab', [pair[::-1] if back else pair for pair in pai...  7.85 us
    all_to_all x1, starting transfers between devices, body(): sums = lax.all_to_all(sums.reshape(SLABS, 1, N), 'slab', 0, 0, tiled=True)  7.44 us
  transfers between devices with their start and end apart: 7, of which 4 were waited for; matrix products, arithmetic and copies ran while one was open for 0% of the time, Pallas kernels for 3%

profile of v4, /device:TPU:1, one launch (start us, length us, event | category | flops | bytes accessed | tf_op | source)
XLA Modules:
  0.0 65.5 jit_solution(11946393531573159826)
XLA Ops:
  0.6 1.0 %pack_kernel.1 = (f32[8,2,512]{2,1,0:T(2,128)S(1)}, f32[8,2,512]{2,1,0:T(2,128)S(1)}) custom-call(f32[4]{0:T(128)} %refs_0_.1, f32[4,512]{1,0:T(4,128)} %refs_1_.1, f32[4,512]{1,0:T(4,128)} %refs_2_.1, s32[4,512]{1,0:T(4,128)} %refs_3_.1, s32[3,4,512]{2,1,0:T(4,128)} %refs_4_.1, f32[3,4,4,512]{3,2,1,0:T(4,128)} %refs_5_.1), custom_call_target="tpu_custom_call" | custom-call | tf_op jit(solution)/shard_map/pack_kernel/pallas_call | solution.py:492
  1.7 3.3 %collective-permute-start = (f32[8,2,512]{2,1,0:T(2,128)S(1)}, f32[8,2,512]{2,1,0:T(2,128)S(1)}, u32[]{:S(2)}, u32[]{:S(2)}) collective-permute-start(f32[8,2,512]{2,1,0:T(2,128)S(1)} %get-tuple-element.13), channel_id=1, source_target_pairs={{0,1},{1,0},{2,3},{3,2},{4,5},{5,4},{6,7},{7,6},{8,9},{9,8},{10,11... | collective-permute-start | bytes 98312 | tf_op jit(solution)/shard_map/ppermute | solution.py:504
  5.0 0.0 collective-permute-start.2
  5.0 0.7 %collective-permute-start.1 = (f32[8,2,512]{2,1,0:T(2,128)S(1)}, f32[8,2,512]{2,1,0:T(2,128)S(1)}, u32[]{:S(2)}, u32[]{:S(2)}) collective-permute-start(f32[8,2,512]{2,1,0:T(2,128)S(1)} %get-tuple-element.12.own_ref), channel_id=1, source_target_pairs={{0,2},{1,3},{2,4},{3,5},{4,6},{5,7},{6,8},{7,9},{8,10},{9,11},{10,... | collective-permute-start | bytes 98312 | tf_op jit(solution)/shard_map/ppermute | solution.py:504
  5.6 0.2 collective-permute-done.near_ref
  5.8 1.7 %chip_spread_kernel.1 = (f32[2,4,128,128]{3,2,1,0:T(8,128)S(1)}, f32[128,512]{1,0:T(8,128)S(1)}) custom-call(f32[8,2,512]{2,1,0:T(2,128)S(1)} %get-tuple-element.12.own_ref, f32[8,2,512]{2,1,0:T(2,128)S(1)} %collective-permute-done.near_ref), custom_call_target="tpu_custom_call" | custom-call | tf_op jit(solution)/shard_map/chip_spread_kernel/pallas_call | solution.py:492
  7.5 5.1 %collective-permute-done.2.cross_ref = f32[8,2,512]{2,1,0:T(2,128)S(1)} collective-permute-done((f32[8,2,512]{2,1,0:T(2,128)S(1)}, f32[8,2,512]{2,1,0:T(2,128)S(1)}, u32[]{:S(2)}, u32[]{:S(2)}) %collective-permute-start.2) | collective-permute-done | bytes 32800 | tf_op jit(solution)/shard_map/ppermute | solution.py:504
  12.6 0.0 collective-permute-done.1.same_ref
  12.6 2.1 %spread_kernel.1 = f32[32,4,8,128]{3,2,1,0:T(8,128)S(1)} custom-call(f32[2,4,128,128]{3,2,1,0:T(8,128)S(1)} %get-tuple-element.14.chip_ref, f32[8,2,512]{2,1,0:T(2,128)S(1)} %collective-permute-done.1.same_ref, f32[8,2,512]{2,1,0:T(2,128)S(1)} %collective-permute-done.2.cross_ref, bf16[2,256,256]{2,1,0:T(8,128)(2,1)} %constant.8.clone.y_hbm.inverse_ref, ...), custom_call_target="tpu_custom_call" | custom-call | tf_op jit(solution)/shard_map/spread_kernel/pallas_call | solution.py:492
  14.8 0.0 copy-start
  14.8 0.0 copy-start.1
  14.8 14.0 %all_to_all.15 = f32[32,32,128]{2,1,0:T(8,128)S(1)} all-to-all(f32[32,32,128]{2,1,0:T(8,128)S(1)} %bitcast.10), channel_id=1, replica_groups={{0,2,4,6,8,10,12,14,16,18,20,22,24,26,28,30,32,34,36,38,40,42,44,46,48,..., dimensions={0} | all-to-all | bytes 1048576 | tf_op jit(solution)/shard_map/all_to_all | solution.py:514
  28.7 0.0 copy-done
  28.8 0.0 copy-done.1
  28.8 0.8 %column_kernel.1 = f32[1024,128]{1,0:T(8,128)S(1)} custom-call(f32[1024,128]{1,0:T(8,128)S(1)} %bitcast.8, f32[128,512]{1,0:T(8,128)S(1)} %get-tuple-element.15.influence_ref, bf16[2,256,256]{2,1,0:T(8,128)(2,1)S(1)} %copy-done.1, bf16[2,256,256]{2,1,0:T(8,128)(2,1)S(1)} %copy-done), custom_call_target="tpu_custom_call" | custom-call | tf_op jit(solution)/shard_map/column_kernel/pallas_call | solution.py:492
  29.6 0.0 copy-start.2
  29.6 13.3 %all_to_all.16 = f32[32,32,128]{2,1,0:T(8,128)S(1)} all-to-all(f32[32,32,128]{2,1,0:T(8,128)S(1)} %bitcast.9), channel_id=1, replica_groups={{0,2,4,6,8,10,12,14,16,18,20,22,24,26,28,30,32,34,36,38,40,42,44,46,48,..., dimensions={0} | all-to-all | bytes 1048576 | tf_op jit(solution)/shard_map/all_to_all | solution.py:514
  42.9 0.0 copy-done.2
  42.9 4.9 %sample_kernel.1 = (f32[3,2,512]{2,1,0:T(2,128)S(1)}, f32[3,2,512]{2,1,0:T(2,128)S(1)}, f32[3,2,512]{2,1,0:T(2,128)S(1)}, f32[3,2,512]{2,1,0:T(2,128)S(1)}, f32[64,128]{1,0:T(8,128)}) custom-call(f32[32,4,8,128]{3,2,1,0:T(8,128)S(1)} %bitcast.11, f32[8,2,512]{2,1,0:T(2,128)S(1)} %get-tuple-element.12.own_ref, ...), custom_call_target="tpu_custom_call" | custom-call | tf_op jit(solution)/shard_map/sample_kernel/pallas_call | solution.py:492
  47.8 7.4 %all-to-all-start.2 = ((f32[64,1,128]{2,1,0:T(1,128)}), f32[64,1,128]{2,1,0:T(1,128)S(1)}, u32[]{:S(2)}, u32[]{:S(2)}) async-start(f32[64,1,128]{2,1,0:T(1,128)} %bitcast.5), calls=%async_computation.2 | async-start | bytes 65536 | tf_op jit(solution)/shard_map/all_to_all | solution.py:581
  55.3 0.7 collective-permute-start.3
  55.9 5.8 %collective-permute-start.4 = (f32[3,2,512]{2,1,0:T(2,128)S(1)}, f32[3,2,512]{2,1,0:T(2,128)S(1)}, u32[]{:S(2)}, u32[]{:S(2)}) collective-permute-start(f32[3,2,512]{2,1,0:T(2,128)S(1)} %get-tuple-element.18), channel_id=1, source_target_pairs={{2,0},{3,1},{4,2},{5,3},{6,4},{7,5},{8,6},{9,7},{10,8},{11,9},{12,... | collective-permute-start | bytes 36872 | tf_op jit(solution)/shard_map/ppermute | solution.py:504
  61.7 0.6 collective-permute-start.5
  62.3 0.0 collective-permute-done.3.near_ref
  62.3 0.3 collective-permute-done.4.same_ref
  62.6 2.3 %collective-permute-done.5.cross_ref = f32[3,2,512]{2,1,0:T(2,128)S(1)} collective-permute-done((f32[3,2,512]{2,1,0:T(2,128)S(1)}, f32[3,2,512]{2,1,0:T(2,128)S(1)}, u32[]{:S(2)}, u32[]{:S(2)}) %collective-permute-start.5) | collective-permute-done | bytes 12320 | tf_op jit(solution)/shard_map/ppermute | solution.py:504
  64.9 0.0 all-to-all-done.2
  64.9 0.7 %finish_kernel.1 = (f32[3,4,512]{2,1,0:T(4,128)}, f32[4]{0:T(128)}, f32[4]{0:T(128)}) custom-call(f32[3,2,512]{2,1,0:T(2,128)S(1)} %get-tuple-element.16.own_ref, f32[3,2,512]{2,1,0:T(2,128)S(1)} %collective-permute-done.3.near_ref, f32[3,2,512]{2,1,0:T(2,128)S(1)} %collective-permute-done.4.same_ref, f32[3,2,512]{2,1,0:T(2,128)S(1)} %collective-permute-done.5.cross_ref, ...), custom_call_target="tpu_custom_call" | custom-call | tf_op jit(solution)/shard_map/finish_kernel/pallas_call | solution.py:582
Async XLA Ops:
  1.7 4.1 %collective-permute-start = (f32[8,2,512]{2,1,0:T(2,128)S(1)}, f32[8,2,512]{2,1,0:T(2,128)S(1)}, u32[]{:S(2)}, u32[]{:S(2)}) collective-permute-start(f32[8,2,512]{2,1,0:T(2,128)S(1)} %get-tuple-element.13), channel_id=1, source_target_pairs={{0,1},{1,0},{2,3},{3,2},{4,5},{5,4},{6,7},{7,6},{8,9},{9,8},{10,11... | collective-permute-start | bytes 98312 | tf_op jit(solution)/shard_map/ppermute | solution.py:504
  5.0 7.7 %collective-permute-start.2 = (f32[8,2,512]{2,1,0:T(2,128)S(1)}, f32[8,2,512]{2,1,0:T(2,128)S(1)}, u32[]{:S(2)}, u32[]{:S(2)}) collective-permute-start(f32[8,2,512]{2,1,0:T(2,128)S(1)} %get-tuple-element.13), channel_id=1, source_target_pairs={{0,3},{1,2},{2,5},{3,4},{4,7},{5,6},{6,9},{7,8},{8,11},{9,10},{10,... | collective-permute-start | bytes 98312 | tf_op jit(solution)/shard_map/ppermute | solution.py:504
  5.0 7.7 %collective-permute-start.1 = (f32[8,2,512]{2,1,0:T(2,128)S(1)}, f32[8,2,512]{2,1,0:T(2,128)S(1)}, u32[]{:S(2)}, u32[]{:S(2)}) collective-permute-start(f32[8,2,512]{2,1,0:T(2,128)S(1)} %get-tuple-element.12.own_ref), channel_id=1, source_target_pairs={{0,2},{1,3},{2,4},{3,5},{4,6},{5,7},{6,8},{7,9},{8,10},{9,11},{10,... | collective-permute-start | bytes 98312 | tf_op jit(solution)/shard_map/ppermute | solution.py:504
  14.8 14.0 %copy-start = (bf16[2,256,256]{2,1,0:T(8,128)(2,1)S(1)}, bf16[2,256,256]{2,1,0:T(8,128)(2,1)}, u32[]{:S(2)}) copy-start(bf16[2,256,256]{2,1,0:T(8,128)(2,1)} %constant.8.clone.y_hbm.inverse_ref) | copy-start | bytes 786436
  14.8 14.0 %copy-start.1 = (bf16[2,256,256]{2,1,0:T(8,128)(2,1)S(1)}, bf16[2,256,256]{2,1,0:T(8,128)(2,1)}, u32[]{:S(2)}) copy-start(bf16[2,256,256]{2,1,0:T(8,128)(2,1)} %constant.10.clone.forward_ref.y_ref) | copy-start | bytes 786436
  29.6 13.4 %copy-start.2 = (bf16[2,256,256]{2,1,0:T(8,128)(2,1)S(1)}, bf16[2,256,256]{2,1,0:T(8,128)(2,1)}, u32[]{:S(2)}) copy-start(bf16[2,256,256]{2,1,0:T(8,128)(2,1)} %constant.11.clone.x_ref) | copy-start | bytes 786436
  47.8 17.1 %all-to-all-start.2 = ((f32[64,1,128]{2,1,0:T(1,128)}), f32[64,1,128]{2,1,0:T(1,128)S(1)}, u32[]{:S(2)}, u32[]{:S(2)}) async-start(f32[64,1,128]{2,1,0:T(1,128)} %bitcast.5), calls=%async_computation.2 | async-start | bytes 65536 | tf_op jit(solution)/shard_map/all_to_all | solution.py:581
  55.3 7.0 %collective-permute-start.3 = (f32[3,2,512]{2,1,0:T(2,128)S(1)}, f32[3,2,512]{2,1,0:T(2,128)S(1)}, u32[]{:S(2)}, u32[]{:S(2)}) collective-permute-start(f32[3,2,512]{2,1,0:T(2,128)S(1)} %get-tuple-element.17), channel_id=1, source_target_pairs={{1,0},{0,1},{3,2},{2,3},{5,4},{4,5},{7,6},{6,7},{9,8},{8,9},{11,10... | collective-permute-start | bytes 36872 | tf_op jit(solution)/shard_map/ppermute | solution.py:504
  55.9 6.6 %collective-permute-start.4 = (f32[3,2,512]{2,1,0:T(2,128)S(1)}, f32[3,2,512]{2,1,0:T(2,128)S(1)}, u32[]{:S(2)}, u32[]{:S(2)}) collective-permute-start(f32[3,2,512]{2,1,0:T(2,128)S(1)} %get-tuple-element.18), channel_id=1, source_target_pairs={{2,0},{3,1},{4,2},{5,3},{6,4},{7,5},{8,6},{9,7},{10,8},{11,9},{12,... | collective-permute-start | bytes 36872 | tf_op jit(solution)/shard_map/ppermute | solution.py:504
  61.7 3.1 %collective-permute-start.5 = (f32[3,2,512]{2,1,0:T(2,128)S(1)}, f32[3,2,512]{2,1,0:T(2,128)S(1)}, u32[]{:S(2)}, u32[]{:S(2)}) collective-permute-start(f32[3,2,512]{2,1,0:T(2,128)S(1)} %get-tuple-element.19), channel_id=1, source_target_pairs={{3,0},{2,1},{5,2},{4,3},{7,4},{6,5},{9,6},{8,7},{11,8},{10,9},{13,... | collective-permute-start | bytes 36872 | tf_op jit(solution)/shard_map/ppermute | solution.py:504

commit v5 on v4

--- a/solution.py
+++ b/solution.py
@@ -279,20 +279,22 @@
     spread_planes([(BELOW, below), (FAR, far)], keep, planes)
     for copy in copies:
         copy.wait()
-    stacked = jnp.concatenate(
-        [jnp.concatenate([planes[0][p], planes[1][p]], axis=1) for p in range(DEEP)], axis=0
-    )
-    turned = times_table(stacked, y_ref)
-    upright = jnp.concatenate(
-        [
-            jnp.concatenate([turned[b * N : b * N + N, :N], turned[b * N : b * N + N, N:]], axis=0)
-            for b in range(DEEP)
-        ],
-        axis=1,
-    )
-    columns = table_times(x_ref, upright)
-    for b in range(DEEP):
-        out_ref[:, b] = columns[:, b * N : b * N + N].reshape(N // 4, 8, N)
+    for first in range(0, DEEP, 2):
+        stacked = jnp.concatenate(
+            [jnp.concatenate([planes[0][p], planes[1][p]], axis=1) for p in (first, first + 1)],
+            axis=0,
+        )
+        turned = times_table(stacked, y_ref)
+        upright = jnp.concatenate(
+            [
+                jnp.concatenate([turned[b : b + N, :N], turned[b : b + N, N:]], axis=0)
+                for b in (0, N)
+            ],
+            axis=1,
+        )
+        columns = table_times(x_ref, upright)
+        for b in range(2):
+            out_ref[:, first + b] = columns[:, b * N : b * N + N].reshape(N // 4, 8, N)
 
 
 def frequency(counter):
@@ -366,16 +368,21 @@
     sums,
 ):
     core = lax.rem(lax.axis_index("slab"), 2)
-    columns = jnp.concatenate([in_ref[:, b].reshape(2 * N, N) for b in range(DEEP)], axis=1)
-    upright = table_times(x_ref, columns)
-    flat = jnp.concatenate(
-        [
-            jnp.concatenate([upright[:N, b * N : b * N + N], upright[N:, b * N : b * N + N]], axis=1)
-            for b in range(DEEP)
-        ],
-        axis=0,
-    )
-    pairs = times_table(flat, y_ref)
+    pairs = []
+    for first in range(0, DEEP, 2):
+        columns = jnp.concatenate(
+            [in_ref[:, b].reshape(2 * N, N) for b in (first, first + 1)], axis=1
+        )
+        upright = table_times(x_ref, columns)
+        flat = jnp.concatenate(
+            [
+                jnp.concatenate([upright[:N, b : b + N], upright[N:, b : b + N]], axis=1)
+                for b in (0, N)
+            ],
+            axis=0,
+        )
+        pairs.append(times_table(flat, y_ref))
+    pairs = jnp.concatenate(pairs, axis=0)
     lower, upper = by_core(core, own_ref, near_ref)
     far, below = by_core(core, same_ref, cross_ref)
     sources = ((LOWER, lower), (UPPER, upper), (BELOW, below), (FAR, far))

time: 65.8 us -> 65.6 us (level)
  no operation moved by 1% of the time
where the time goes in v5:
time: 65.6 us; the launch traced here: 65.4 us
  blocking collectives  27.3 us (42%)
  starting transfers between devices  18.4 us (28%)
  Pallas kernels  11.1 us (17%)
  waiting for transfers between devices  7.86 us (12%)
  between operations  0.7 us (1%)
    all_to_all x2, blocking collectives, exchanged(): lax.all_to_all(value, 'slab', 0, 0, tiled=True, axis_index_groups=CORES)  27.3 us
    ppermute x6, starting transfers between devices, moved(): lax.ppermute(value, 'slab', [pair[::-1] if back else pair for pair in pai...  11 us
    pallas_call x5, Pallas kernels, run(): pl.pallas_call(kernel, out_shape=out_shape, in_specs=in_specs, out_specs=...  10.4 us
    ppermute x6, waiting for transfers between devices, moved(): lax.ppermute(value, 'slab', [pair[::-1] if back else pair for pair in pai...  7.85 us
    all_to_all x1, starting transfers between devices, body(): sums = lax.all_to_all(sums.reshape(SLABS, 1, N), 'slab', 0, 0, tiled=True)  7.44 us
  transfers between devices with their start and end apart: 7, of which 4 were waited for; matrix products, arithmetic and copies ran while one was open for 0% of the time, Pallas kernels for 3%

profile of v5, /device:TPU:1, one launch (start us, length us, event | category | flops | bytes accessed | tf_op | source)
XLA Modules:
  0.0 65.4 jit_solution(17664563720420418038)
XLA Ops:
  0.6 1.0 %pack_kernel.1 = (f32[8,2,512]{2,1,0:T(2,128)S(1)}, f32[8,2,512]{2,1,0:T(2,128)S(1)}) custom-call(f32[4]{0:T(128)} %refs_0_.1, f32[4,512]{1,0:T(4,128)} %refs_1_.1, f32[4,512]{1,0:T(4,128)} %refs_2_.1, s32[4,512]{1,0:T(4,128)} %refs_3_.1, s32[3,4,512]{2,1,0:T(4,128)} %refs_4_.1, f32[3,4,4,512]{3,2,1,0:T(4,128)} %refs_5_.1), custom_call_target="tpu_custom_call" | custom-call | tf_op jit(solution)/shard_map/pack_kernel/pallas_call | solution.py:499
  1.7 3.3 %collective-permute-start = (f32[8,2,512]{2,1,0:T(2,128)S(1)}, f32[8,2,512]{2,1,0:T(2,128)S(1)}, u32[]{:S(2)}, u32[]{:S(2)}) collective-permute-start(f32[8,2,512]{2,1,0:T(2,128)S(1)} %get-tuple-element.13), channel_id=1, source_target_pairs={{0,1},{1,0},{2,3},{3,2},{4,5},{5,4},{6,7},{7,6},{8,9},{9,8},{10,11... | collective-permute-start | bytes 98312 | tf_op jit(solution)/shard_map/ppermute | solution.py:511
  5.0 0.0 collective-permute-start.2
  5.0 0.7 %collective-permute-start.1 = (f32[8,2,512]{2,1,0:T(2,128)S(1)}, f32[8,2,512]{2,1,0:T(2,128)S(1)}, u32[]{:S(2)}, u32[]{:S(2)}) collective-permute-start(f32[8,2,512]{2,1,0:T(2,128)S(1)} %get-tuple-element.12.own_ref), channel_id=1, source_target_pairs={{0,2},{1,3},{2,4},{3,5},{4,6},{5,7},{6,8},{7,9},{8,10},{9,11},{10,... | collective-permute-start | bytes 98312 | tf_op jit(solution)/shard_map/ppermute | solution.py:511
  5.6 0.2 collective-permute-done.near_ref
  5.8 1.7 %chip_spread_kernel.1 = (f32[2,4,128,128]{3,2,1,0:T(8,128)S(1)}, f32[128,512]{1,0:T(8,128)S(1)}) custom-call(f32[8,2,512]{2,1,0:T(2,128)S(1)} %get-tuple-element.12.own_ref, f32[8,2,512]{2,1,0:T(2,128)S(1)} %collective-permute-done.near_ref), custom_call_target="tpu_custom_call" | custom-call | tf_op jit(solution)/shard_map/chip_spread_kernel/pallas_call | solution.py:499
  7.5 5.1 %collective-permute-done.2.cross_ref = f32[8,2,512]{2,1,0:T(2,128)S(1)} collective-permute-done((f32[8,2,512]{2,1,0:T(2,128)S(1)}, f32[8,2,512]{2,1,0:T(2,128)S(1)}, u32[]{:S(2)}, u32[]{:S(2)}) %collective-permute-start.2) | collective-permute-done | bytes 32800 | tf_op jit(solution)/shard_map/ppermute | solution.py:511
  12.6 0.0 collective-permute-done.1.same_ref
  12.6 2.0 %spread_kernel.1 = f32[32,4,8,128]{3,2,1,0:T(8,128)S(1)} custom-call(f32[2,4,128,128]{3,2,1,0:T(8,128)S(1)} %get-tuple-element.14.chip_ref, f32[8,2,512]{2,1,0:T(2,128)S(1)} %collective-permute-done.1.same_ref, f32[8,2,512]{2,1,0:T(2,128)S(1)} %collective-permute-done.2.cross_ref, bf16[2,256,256]{2,1,0:T(8,128)(2,1)} %constant.8.clone.y_hbm.inverse_ref, ...), custom_call_target="tpu_custom_call" | custom-call | tf_op jit(solution)/shard_map/spread_kernel/pallas_call | solution.py:499
  14.6 0.0 copy-start
  14.7 0.0 copy-start.1
  14.7 14.0 %all_to_all.15 = f32[32,32,128]{2,1,0:T(8,128)S(1)} all-to-all(f32[32,32,128]{2,1,0:T(8,128)S(1)} %bitcast.10), channel_id=1, replica_groups={{0,2,4,6,8,10,12,14,16,18,20,22,24,26,28,30,32,34,36,38,40,42,44,46,48,..., dimensions={0} | all-to-all | bytes 1048576 | tf_op jit(solution)/shard_map/all_to_all | solution.py:521
  28.6 0.0 copy-done
  28.6 0.0 copy-done.1
  28.6 0.8 %column_kernel.1 = f32[1024,128]{1,0:T(8,128)S(1)} custom-call(f32[1024,128]{1,0:T(8,128)S(1)} %bitcast.8, f32[128,512]{1,0:T(8,128)S(1)} %get-tuple-element.15.influence_ref, bf16[2,256,256]{2,1,0:T(8,128)(2,1)S(1)} %copy-done.1, bf16[2,256,256]{2,1,0:T(8,128)(2,1)S(1)} %copy-done), custom_call_target="tpu_custom_call" | custom-call | tf_op jit(solution)/shard_map/column_kernel/pallas_call | solution.py:499
  29.5 0.0 copy-start.2
  29.5 13.3 %all_to_all.16 = f32[32,32,128]{2,1,0:T(8,128)S(1)} all-to-all(f32[32,32,128]{2,1,0:T(8,128)S(1)} %bitcast.9), channel_id=1, replica_groups={{0,2,4,6,8,10,12,14,16,18,20,22,24,26,28,30,32,34,36,38,40,42,44,46,48,..., dimensions={0} | all-to-all | bytes 1048576 | tf_op jit(solution)/shard_map/all_to_all | solution.py:521
  42.8 0.0 copy-done.2
  42.8 4.8 %sample_kernel.1 = (f32[3,2,512]{2,1,0:T(2,128)S(1)}, f32[3,2,512]{2,1,0:T(2,128)S(1)}, f32[3,2,512]{2,1,0:T(2,128)S(1)}, f32[3,2,512]{2,1,0:T(2,128)S(1)}, f32[64,128]{1,0:T(8,128)}) custom-call(f32[32,4,8,128]{3,2,1,0:T(8,128)S(1)} %bitcast.11, f32[8,2,512]{2,1,0:T(2,128)S(1)} %get-tuple-element.12.own_ref, ...), custom_call_target="tpu_custom_call" | custom-call | tf_op jit(solution)/shard_map/sample_kernel/pallas_call | solution.py:499
  47.7 7.4 %all-to-all-start.2 = ((f32[64,1,128]{2,1,0:T(1,128)}), f32[64,1,128]{2,1,0:T(1,128)S(1)}, u32[]{:S(2)}, u32[]{:S(2)}) async-start(f32[64,1,128]{2,1,0:T(1,128)} %bitcast.5), calls=%async_computation.2 | async-start | bytes 65536 | tf_op jit(solution)/shard_map/all_to_all | solution.py:588
  55.1 0.7 %collective-permute-start.3 = (f32[3,2,512]{2,1,0:T(2,128)S(1)}, f32[3,2,512]{2,1,0:T(2,128)S(1)}, u32[]{:S(2)}, u32[]{:S(2)}) collective-permute-start(f32[3,2,512]{2,1,0:T(2,128)S(1)} %get-tuple-element.17), channel_id=1, source_target_pairs={{1,0},{0,1},{3,2},{2,3},{5,4},{4,5},{7,6},{6,7},{9,8},{8,9},{11,10... | collective-permute-start | bytes 36872 | tf_op jit(solution)/shard_map/ppermute | solution.py:511
  55.8 5.8 %collective-permute-start.4 = (f32[3,2,512]{2,1,0:T(2,128)S(1)}, f32[3,2,512]{2,1,0:T(2,128)S(1)}, u32[]{:S(2)}, u32[]{:S(2)}) collective-permute-start(f32[3,2,512]{2,1,0:T(2,128)S(1)} %get-tuple-element.18), channel_id=1, source_target_pairs={{2,0},{3,1},{4,2},{5,3},{6,4},{7,5},{8,6},{9,7},{10,8},{11,9},{12,... | collective-permute-start | bytes 36872 | tf_op jit(solution)/shard_map/ppermute | solution.py:511
  61.6 0.6 collective-permute-start.5
  62.1 0.0 collective-permute-done.3.near_ref
  62.1 0.3 collective-permute-done.4.same_ref
  62.4 2.3 %collective-permute-done.5.cross_ref = f32[3,2,512]{2,1,0:T(2,128)S(1)} collective-permute-done((f32[3,2,512]{2,1,0:T(2,128)S(1)}, f32[3,2,512]{2,1,0:T(2,128)S(1)}, u32[]{:S(2)}, u32[]{:S(2)}) %collective-permute-start.5) | collective-permute-done | bytes 12320 | tf_op jit(solution)/shard_map/ppermute | solution.py:511
  64.7 0.0 all-to-all-done.2
  64.7 0.7 %finish_kernel.1 = (f32[3,4,512]{2,1,0:T(4,128)}, f32[4]{0:T(128)}, f32[4]{0:T(128)}) custom-call(f32[3,2,512]{2,1,0:T(2,128)S(1)} %get-tuple-element.16.own_ref, f32[3,2,512]{2,1,0:T(2,128)S(1)} %collective-permute-done.3.near_ref, f32[3,2,512]{2,1,0:T(2,128)S(1)} %collective-permute-done.4.same_ref, f32[3,2,512]{2,1,0:T(2,128)S(1)} %collective-permute-done.5.cross_ref, ...), custom_call_target="tpu_custom_call" | custom-call | tf_op jit(solution)/shard_map/finish_kernel/pallas_call | solution.py:589
Async XLA Ops:
  1.7 4.1 %collective-permute-start = (f32[8,2,512]{2,1,0:T(2,128)S(1)}, f32[8,2,512]{2,1,0:T(2,128)S(1)}, u32[]{:S(2)}, u32[]{:S(2)}) collective-permute-start(f32[8,2,512]{2,1,0:T(2,128)S(1)} %get-tuple-element.13), channel_id=1, source_target_pairs={{0,1},{1,0},{2,3},{3,2},{4,5},{5,4},{6,7},{7,6},{8,9},{9,8},{10,11... | collective-permute-start | bytes 98312 | tf_op jit(solution)/shard_map/ppermute | solution.py:511
  5.0 7.7 %collective-permute-start.2 = (f32[8,2,512]{2,1,0:T(2,128)S(1)}, f32[8,2,512]{2,1,0:T(2,128)S(1)}, u32[]{:S(2)}, u32[]{:S(2)}) collective-permute-start(f32[8,2,512]{2,1,0:T(2,128)S(1)} %get-tuple-element.13), channel_id=1, source_target_pairs={{0,3},{1,2},{2,5},{3,4},{4,7},{5,6},{6,9},{7,8},{8,11},{9,10},{10,... | collective-permute-start | bytes 98312 | tf_op jit(solution)/shard_map/ppermute | solution.py:511
  5.0 7.7 %collective-permute-start.1 = (f32[8,2,512]{2,1,0:T(2,128)S(1)}, f32[8,2,512]{2,1,0:T(2,128)S(1)}, u32[]{:S(2)}, u32[]{:S(2)}) collective-permute-start(f32[8,2,512]{2,1,0:T(2,128)S(1)} %get-tuple-element.12.own_ref), channel_id=1, source_target_pairs={{0,2},{1,3},{2,4},{3,5},{4,6},{5,7},{6,8},{7,9},{8,10},{9,11},{10,... | collective-permute-start | bytes 98312 | tf_op jit(solution)/shard_map/ppermute | solution.py:511
  14.6 14.0 %copy-start = (bf16[2,256,256]{2,1,0:T(8,128)(2,1)S(1)}, bf16[2,256,256]{2,1,0:T(8,128)(2,1)}, u32[]{:S(2)}) copy-start(bf16[2,256,256]{2,1,0:T(8,128)(2,1)} %constant.8.clone.y_hbm.inverse_ref) | copy-start | bytes 786436
  14.7 14.0 %copy-start.1 = (bf16[2,256,256]{2,1,0:T(8,128)(2,1)S(1)}, bf16[2,256,256]{2,1,0:T(8,128)(2,1)}, u32[]{:S(2)}) copy-start(bf16[2,256,256]{2,1,0:T(8,128)(2,1)} %constant.10.clone.forward_ref.y_ref) | copy-start | bytes 786436
  29.5 13.4 %copy-start.2 = (bf16[2,256,256]{2,1,0:T(8,128)(2,1)S(1)}, bf16[2,256,256]{2,1,0:T(8,128)(2,1)}, u32[]{:S(2)}) copy-start(bf16[2,256,256]{2,1,0:T(8,128)(2,1)} %constant.11.clone.x_ref) | copy-start | bytes 786436
  47.7 17.1 %all-to-all-start.2 = ((f32[64,1,128]{2,1,0:T(1,128)}), f32[64,1,128]{2,1,0:T(1,128)S(1)}, u32[]{:S(2)}, u32[]{:S(2)}) async-start(f32[64,1,128]{2,1,0:T(1,128)} %bitcast.5), calls=%async_computation.2 | async-start | bytes 65536 | tf_op jit(solution)/shard_map/all_to_all | solution.py:588
  55.1 7.0 %collective-permute-start.3 = (f32[3,2,512]{2,1,0:T(2,128)S(1)}, f32[3,2,512]{2,1,0:T(2,128)S(1)}, u32[]{:S(2)}, u32[]{:S(2)}) collective-permute-start(f32[3,2,512]{2,1,0:T(2,128)S(1)} %get-tuple-element.17), channel_id=1, source_target_pairs={{1,0},{0,1},{3,2},{2,3},{5,4},{4,5},{7,6},{6,7},{9,8},{8,9},{11,10... | collective-permute-start | bytes 36872 | tf_op jit(solution)/shard_map/ppermute | solution.py:511
  55.8 6.6 %collective-permute-start.4 = (f32[3,2,512]{2,1,0:T(2,128)S(1)}, f32[3,2,512]{2,1,0:T(2,128)S(1)}, u32[]{:S(2)}, u32[]{:S(2)}) collective-permute-start(f32[3,2,512]{2,1,0:T(2,128)S(1)} %get-tuple-element.18), channel_id=1, source_target_pairs={{2,0},{3,1},{4,2},{5,3},{6,4},{7,5},{8,6},{9,7},{10,8},{11,9},{12,... | collective-permute-start | bytes 36872 | tf_op jit(solution)/shard_map/ppermute | solution.py:511
  61.6 3.1 %collective-permute-start.5 = (f32[3,2,512]{2,1,0:T(2,128)S(1)}, f32[3,2,512]{2,1,0:T(2,128)S(1)}, u32[]{:S(2)}, u32[]{:S(2)}) collective-permute-start(f32[3,2,512]{2,1,0:T(2,128)S(1)} %get-tuple-element.19), channel_id=1, source_target_pairs={{3,0},{2,1},{5,2},{4,3},{7,4},{6,5},{9,6},{8,7},{11,8},{10,9},{13,... | collective-permute-start | bytes 36872 | tf_op jit(solution)/shard_map/ppermute | solution.py:511
